TPU v7x, 256 devices: a whole 4x4x8 slice. The times are simulated.
256 devices in a mesh: section: 8 (over z_lo, x), dp: 32 (over z_hi, y, core).
Axes of the slice: x: 4, y: 4, z: 8 (z_hi: 4, z_lo: 2; z = z_hi * 2 + z_lo), core: 2. Of those that a mesh axis runs over, the one named last changes fastest.
Arguments:
- ln_input: bfloat16 [8, 4096, 12288], P('section', 'dp'), may hold values from -6 to 6
- ln_grad: bfloat16 [8, 4096, 12288], P('section', 'dp'), may hold values from -6 to 6
- top_grad: bfloat16 [8, 4096, 12288], P('section', 'dp'), may hold values from -6 to 6
- ln_gain: float32 [8, 12288], P('section'), may hold values from 0.1 to 1.9
- hidden: bfloat16 [8, 4096, 64], P('section', 'dp'), may hold values from -8 to 8
- master: float32 [8, 64, 12288], P('section', 'dp'), may hold values from -6 to 6
- moment: float32 [8, 64, 12288], P('section', 'dp'), may hold values from -6 to 6
- second: float32 [8, 64, 12288], P('section', 'dp'), may hold values from 0.1 to 4
Outputs:
- new_master: float32 [8, 64, 12288], P('section', 'dp')
- new_moment: float32 [8, 64, 12288], P('section', 'dp')
- new_second: float32 [8, 64, 12288], P('section', 'dp')
- weights: bfloat16 [8, 64, 12288], P('section')
All inputs are finite; a program needn't handle non-finite values.
Results may differ from a plain program's by a relative error of at most 0.0078.
Values may be sent and summed in bfloat16 or wider, within the bound.
No kernel may reach another device: no remote copies, remote signals or barrier semaphores. Data moves between devices by JAX's collectives and lax.ppermute only.
A program may use at most 64 MiB of HBM per device.

v0:
```python
import jax
import jax.numpy as jnp
from jax import lax
from jax.sharding import Mesh
from jax.sharding import PartitionSpec as P

STEP = 20
DP = ("dp_0", "dp_1", "dp_2")


def shifted_2(value, axis, steps):
    count = lax.axis_size(axis)
    first, last = (max(0, -steps), min(count, count - steps))
    return lax.ppermute(value, axis, [(source, source + steps) for source in range(first, last)])


def split_up(x, dim, devices):
    before, after = (x.shape[:dim], x.shape[dim + 1 :])
    return jnp.moveaxis(x.reshape(*before, devices, -1, *after), dim, 0)


def sent_and_summed(x, axis, dim):
    devices = lax.axis_size(axis)
    blocks = lax.all_to_all(split_up(x, dim, devices), axis, 0, 0, tiled=True)
    return jnp.sum(blocks.astype(jnp.float32), axis=0)


def summed_rows(x, axes, dim):
    far, near = axes
    own = sent_and_summed(split_up(x, dim, lax.axis_size(far)), near, dim + 1)
    return jnp.sum(
        lax.all_to_all(own.astype(jnp.bfloat16), far, 0, 0, tiled=True).astype(jnp.float32), axis=0
    )


def from_everyone(x, axis):
    copies = jnp.broadcast_to(x, (lax.axis_size(axis), *x.shape))
    return lax.all_to_all(copies, axis, split_axis=0, concat_axis=0, tiled=True)


def in_order(blocks, dim):
    blocks = jnp.moveaxis(blocks, 0, dim)
    shape = blocks.shape
    return blocks.reshape(*shape[:dim], shape[dim] * shape[dim + 1], *shape[dim + 2 :])


def gather_axes(x, axes, dim):
    far, near = axes
    first = from_everyone(x, far)
    blocks = jnp.swapaxes(from_everyone(first, near), 0, 1)
    return in_order(blocks.reshape(-1, *x.shape), dim)


def layer_back(ln_input, ln_grad, top_grad, ln_gain):
    values = ln_input.astype(jnp.float32)
    row_mean = jnp.mean(values, axis=-1, keepdims=True)
    centred = values - row_mean
    inv_std = 1.0 / jnp.sqrt(jnp.mean(centred * centred, axis=-1, keepdims=True) + 1e-05)
    normed = centred * inv_std
    scaled = ln_grad.astype(jnp.float32) * ln_gain[:, None, :]
    inner = (
        scaled
        - jnp.mean(scaled, axis=-1, keepdims=True)
        - normed * jnp.mean(scaled * normed, axis=-1, keepdims=True)
    )
    return (top_grad.astype(jnp.float32) + inner * inv_std).astype(jnp.bfloat16)


def adam_update(grad, master, moment, second):
    new_moment = 0.9 * moment + 0.1 * grad
    new_second = 0.95 * second + 0.05 * grad * grad
    first_fix = 1.0 - 0.9**STEP
    second_fix = 1.0 - 0.95**STEP
    update = new_moment / first_fix / (jnp.sqrt(new_second / second_fix) + 1e-08)
    new_master = master - 0.05 * (update + 0.1 * master)
    return (new_master, new_moment, new_second)


def term_maker(columns, received):
    return lax.dot_general(
        columns, received, (((0,), (0,)), ((), ())), preferred_element_type=jnp.float32
    )


def owner_columns(columns, group_size, row_dev, first, last_row):
    tokens_here = columns.shape[0]
    grouped = columns.reshape(tokens_here, group_size, row_dev)
    return grouped.reshape(tokens_here, group_size * (last_row - first))


def shards(ln_input, ln_grad, top_grad, ln_gain, hidden, master, moment, second):
    passed = layer_back(ln_input, ln_grad, top_grad, ln_gain)
    is_last = lax.axis_index("section") == lax.axis_size("section") - 1
    row_dev = master.shape[1]
    width = master.shape[2]
    group_size = lax.axis_size(DP)
    own_cols = hidden[0]
    shifted = shifted_2(passed, "section", -1)
    received = jnp.where(is_last, top_grad, shifted)[0]
    bounds = (0, row_dev)
    first, last_row = bounds
    count = last_row - first
    cols = owner_columns(own_cols, group_size, row_dev, first, last_row)
    grad = summed_rows(
        term_maker(cols, received).astype(jnp.bfloat16), (("dp_0", "dp_1"), "dp_2"), 0
    )
    state = adam_update(
        grad, master[0, first:last_row], moment[0, first:last_row], second[0, first:last_row]
    )
    masters = state[0]
    moments = state[1]
    seconds = state[2]
    pieces = gather_axes(state[0].astype(jnp.bfloat16), (("dp_0", "dp_1"), "dp_2"), 0)
    gathered = pieces.reshape(group_size, count, width)
    weights = gathered.reshape(group_size * row_dev, width)
    return (masters[None], moments[None], seconds[None], weights[None])


def solution(mesh):
    finer = Mesh(
        mesh.devices.reshape(mesh.shape["section"], 4, 4, 2), ("section", "dp_0", "dp_1", "dp_2")
    )
    return jax.shard_map(
        shards,
        mesh=finer,
        in_specs=(
            P("section", DP, None),
            P("section", DP, None),
            P("section", DP, None),
            P("section", None),
            P("section", DP, None),
            P("section", DP, None),
            P("section", DP, None),
            P("section", DP, None),
        ),
        out_specs=(
            P("section", DP, None),
            P("section", DP, None),
            P("section", DP, None),
            P("section", None, None),
        ),
        check_vma=False,
    )
```

profile of v0, /device:TPU:37, one launch (start us, length us, event | category | flops | bytes accessed | tf_op | source)
XLA Modules:
  0.0 172.2 jit_solution(5630410384963327978)
XLA Ops:
  0.6 0.0 copy-start
  0.6 0.0 copy-start.1
  0.7 0.0 copy-start.2
  0.7 2.5 %convert_reduce_fusion = f32[128]{0:T(128)S(1)} fusion(bf16[1,128,12288]{2,1,0:T(8,128)(2,1)} %param.8), kind=kLoop, calls=%fused_computation.3 | loop fusion | flops 3145600 | bytes 3146240 | tf_op jit(solution)/shard_map/reduce_sum | solution.py:56
  3.2 0.3 copy-done.1
  3.5 1.0 fusion.10
  4.5 0.0 copy-done.2
  4.5 0.0 copy-start.3
  4.5 0.0 copy-start.7
  4.5 3.1 %fusion.11 = (f32[128]{0:T(128)S(1)}, f32[128]{0:T(128)S(1)}) fusion(bf16[1,128,12288]{2,1,0:T(8,128)(2,1)S(1)} %copy-done.2, f32[12288]{0:T(1024)} %bitcast.47, f32[128]{0:T(128)S(1)} %add_rsqrt_fusion, f32[128]{0:T(128)S(1)} %broadcast_multiply_fusion.1, bf16[1,128,12288]{2,1,0:T(8,128)(2,1)S(1)} %copy-done.1), kind=kLoop, calls=%fused_computation.15 | loop fusion | flops 12582656 | bytes 6342656 | tf_op jit(solution)/shard_map/reduce_sum | solution.py:63
  7.6 0.0 copy-done.3
  7.7 0.0 copy-done.7
  7.7 3.7 %fusion.9 = bf16[1,128,12288]{2,1,0:T(8,128)(2,1)} fusion(bf16[1,128,12288]{2,1,0:T(8,128)(2,1)S(1)} %copy-done.1, bf16[1,128,12288]{2,1,0:T(8,128)(2,1)S(1)} %copy-done.2, bf16[1,128,12288]{2,1,0:T(8,128)(2,1)S(1)} %copy-done.3, f32[128]{0:T(128)S(1)} %get-tuple-element.9, f32[128]{0:T(128)S(1)} %add_rsqrt_fusion, f32[128]{0:T(128)S(1)} %broadcast_multiply_fusion.1, ...), kind=kLoop, calls=%fused_computation.12 | loop fusion | flops 18874368 | bytes 12634112 | tf_op jit(solution)/shard_map/convert_element_type | solution.py:66
  11.4 2.2 %collective-permute-start = (bf16[1,128,12288]{2,1,0:T(8,128)(2,1)}, bf16[1,128,12288]{2,1,0:T(8,128)(2,1)}, u32[]{:S(2)}, u32[]{:S(2)}) collective-permute-start(bf16[1,128,12288]{2,1,0:T(8,128)(2,1)} %fusion.9), channel_id=1, source_target_pairs={{32,0},{64,32},{96,64},{128,96},{160,128},{192,160},{224,192},{33,... | collective-permute-start | bytes 9437192 | tf_op jit(solution)/shard_map/ppermute | solution.py:14
  13.5 69.0 %collective-permute-done = bf16[1,128,12288]{2,1,0:T(8,128)(2,1)} collective-permute-done((bf16[1,128,12288]{2,1,0:T(8,128)(2,1)}, bf16[1,128,12288]{2,1,0:T(8,128)(2,1)}, u32[]{:S(2)}, u32[]{:S(2)}) %collective-permute-start) | collective-permute-done | bytes 3145760 | tf_op jit(solution)/shard_map/ppermute | solution.py:14
  82.5 0.0 copy-done
  82.5 3.8 %fusion = bf16[64,12288]{1,0:T(8,128)(2,1)} fusion(bf16[1,128,12288]{2,1,0:T(8,128)(2,1)S(1)} %copy-done.3, bf16[1,128,12288]{2,1,0:T(8,128)(2,1)} %collective-permute-done, pred[]{:T(512)S(6)} %eq.3, bf16[1,128,64]{1,2,0:T(8,128)(2,1)S(1)} %copy-done), kind=kOutput, calls=%fused_computation.1 | convolution fusion | flops 203685888 | bytes 7880705 | tf_op jit(solution)/shard_map/dot_general | solution.py:80
  86.4 3.4 %reshape_reshape.3 = bf16[16,2,2,12288]{3,2,1,0:T(2,128)(2,1)S(1)} reshape(bf16[64,12288]{1,0:T(8,128)(2,1)} %fusion) | data formatting | bytes 3145728 | tf_op jit(solution)/shard_map/reshape;reshape | solution.py:19
  89.8 1.3 copy.25
  91.1 6.2 %all_to_all.20 = bf16[2,16,2,12288]{3,2,1,0:T(2,128)(2,1)S(1)} all-to-all(bf16[2,16,2,12288]{3,2,1,0:T(2,128)(2,1)S(1)} %bitcast.45), channel_id=1, replica_groups=mesh['section'=8,'dp_0'=4,'dp_1'=4,'dp_2'=2] {'dp_2'}, dimensions={0} | all-to-all | bytes 3145728 | tf_op jit(solution)/shard_map/all_to_all | solution.py:24
  97.3 0.0 copy-start.4
  97.3 0.0 copy-start.5
  97.3 0.0 copy-start.6
  97.3 3.3 %reduce_sum.63 = bf16[16,2,12288]{2,1,0:T(2,128)(2,1)S(1)} reduce(bf16[2,16,2,12288]{3,2,1,0:T(2,128)(2,1)S(1)} %all_to_all.20, bf16[]{:T(256)} %constant.30.clone.1), dimensions={0}, to_apply=%region_4.5 | reduce | flops 393216 | bytes 2359298 | tf_op jit(solution)/shard_map/reduce_sum | solution.py:25
  100.6 32.5 %all_to_all.21 = bf16[16,2,12288]{2,1,0:T(2,128)(2,1)S(1)} all-to-all(bf16[16,2,12288]{2,1,0:T(2,128)(2,1)S(1)} %reduce_sum.63), channel_id=1, replica_groups=mesh['section'=8,'dp_0'=4,'dp_1'=4,'dp_2'=2] {'dp_0','dp_1'}, dimensions={0} | all-to-all | bytes 1572864 | tf_op jit(solution)/shard_map/all_to_all | solution.py:32
  133.1 0.7 convert_reduce_fusion.1
  133.8 0.0 copy-done.4
  133.8 0.0 copy-done.5
  133.8 0.0 copy-done.6
  133.8 0.3 fusion.24
  134.2 1.5 broadcast_in_dim.4
  135.7 4.3 %all-to-all-start.2 = ((bf16[16,2,12288]{2,1,0:T(2,128)(2,1)}), bf16[16,2,12288]{2,1,0:T(2,128)(2,1)S(1)}, u32[]{:S(2)}, u32[]{:S(2)}) async-start(bf16[16,2,12288]{2,1,0:T(2,128)(2,1)} %broadcast_in_dim.4), calls=%async_computation.2 | async-start | bytes 1572864 | tf_op jit(solution)/shard_map/all_to_all | solution.py:38
  140.0 1.0 multiply_subtract_fusion
  141.0 18.7 %all-to-all-done.2 = bf16[16,2,12288]{2,1,0:T(2,128)(2,1)S(1)} async-done(((bf16[16,2,12288]{2,1,0:T(2,128)(2,1)}), bf16[16,2,12288]{2,1,0:T(2,128)(2,1)S(1)}, u32[]{:S(2)}, u32[]{:S(2)}) %all-to-all-start.2) | async-done | bytes 786464 | tf_op jit(solution)/shard_map/all_to_all | solution.py:38
  159.7 1.4 broadcast_in_dim.5
  161.1 8.1 %all_to_all.22 = bf16[2,16,2,12288]{3,2,1,0:T(2,128)(2,1)S(1)} all-to-all(bf16[2,16,2,12288]{3,2,1,0:T(2,128)(2,1)S(1)} %broadcast_in_dim.5), channel_id=1, replica_groups=mesh['section'=8,'dp_0'=4,'dp_1'=4,'dp_2'=2] {'dp_2'}, dimensions={0} | all-to-all | bytes 3145728 | tf_op jit(solution)/shard_map/all_to_all | solution.py:38
  169.2 1.4 copy.22
  170.7 1.5 broadcast_in_dim_reshape_reshape_reshape_reshape.3
  (3 shorter events, 0.0 us)
Async XLA Ops:
  0.6 81.9 %copy-start = (bf16[1,128,64]{1,2,0:T(8,128)(2,1)S(1)}, bf16[1,128,64]{1,2,0:T(8,128)(2,1)}, u32[]{:S(2)}) copy-start(bf16[1,128,64]{1,2,0:T(8,128)(2,1)} %param.12) | copy-start | bytes 49156
  0.6 2.8 %copy-start.1 = (bf16[1,128,12288]{2,1,0:T(8,128)(2,1)S(1)}, bf16[1,128,12288]{2,1,0:T(8,128)(2,1)}, u32[]{:S(2)}) copy-start(bf16[1,128,12288]{2,1,0:T(8,128)(2,1)} %param.8) | copy-start | bytes 9437188
  0.7 3.9 %copy-start.2 = (bf16[1,128,12288]{2,1,0:T(8,128)(2,1)S(1)}, bf16[1,128,12288]{2,1,0:T(8,128)(2,1)}, u32[]{:S(2)}) copy-start(bf16[1,128,12288]{2,1,0:T(8,128)(2,1)} %param.9) | copy-start | bytes 9437188
  4.5 3.1 %copy-start.3 = (bf16[1,128,12288]{2,1,0:T(8,128)(2,1)S(1)}, bf16[1,128,12288]{2,1,0:T(8,128)(2,1)}, u32[]{:S(2)}) copy-start(bf16[1,128,12288]{2,1,0:T(8,128)(2,1)} %param.10) | copy-start | bytes 9437188
  4.5 3.1 %copy-start.7 = (f32[1,12288]{1,0:T(1,128)S(1)}, f32[1,12288]{1,0:T(1,128)}, u32[]{:S(2)}) copy-start(f32[1,12288]{1,0:T(1,128)} %param.11) | copy-start | bytes 147460
  11.4 71.2 %collective-permute-start = (bf16[1,128,12288]{2,1,0:T(8,128)(2,1)}, bf16[1,128,12288]{2,1,0:T(8,128)(2,1)}, u32[]{:S(2)}, u32[]{:S(2)}) collective-permute-start(bf16[1,128,12288]{2,1,0:T(8,128)(2,1)} %fusion.9), channel_id=1, source_target_pairs={{32,0},{64,32},{96,64},{128,96},{160,128},{192,160},{224,192},{33,... | collective-permute-start | bytes 9437192 | tf_op jit(solution)/shard_map/ppermute | solution.py:14
  97.3 36.5 %copy-start.4 = (f32[1,2,12288]{2,1,0:T(2,128)S(1)}, f32[1,2,12288]{2,1,0:T(2,128)}, u32[]{:S(2)}) copy-start(f32[1,2,12288]{2,1,0:T(2,128)} %param.13) | copy-start | bytes 294916
  97.3 36.6 %copy-start.5 = (f32[1,2,12288]{2,1,0:T(2,128)S(1)}, f32[1,2,12288]{2,1,0:T(2,128)}, u32[]{:S(2)}) copy-start(f32[1,2,12288]{2,1,0:T(2,128)} %param.14) | copy-start | bytes 294916
  97.3 36.6 %copy-start.6 = (f32[1,2,12288]{2,1,0:T(2,128)S(1)}, f32[1,2,12288]{2,1,0:T(2,128)}, u32[]{:S(2)}) copy-start(f32[1,2,12288]{2,1,0:T(2,128)} %param.15) | copy-start | bytes 294916
  135.7 24.0 %all-to-all-start.2 = ((bf16[16,2,12288]{2,1,0:T(2,128)(2,1)}), bf16[16,2,12288]{2,1,0:T(2,128)(2,1)S(1)}, u32[]{:S(2)}, u32[]{:S(2)}) async-start(bf16[16,2,12288]{2,1,0:T(2,128)(2,1)} %broadcast_in_dim.4), calls=%async_computation.2 | async-start | bytes 1572864 | tf_op jit(solution)/shard_map/all_to_all | solution.py:38
where the time goes:
time: 175 us; the launch traced here: 172 us
  waiting for transfers between devices  87.7 us (50%)
  blocking collectives  46.8 us (27%)
  other arithmetic  15.7 us (9%)
  local copies, waits for them, and re-layouts  10.9 us (6%)
  starting transfers between devices  6.46 us (4%)
  matrix products  3.82 us (2%)
    ppermute x1, waiting for transfers between devices, shifted_2(): lax.ppermute(value, axis, [(source, source + steps) for source in range(f...  69 us
    all_to_all x1, blocking collectives, summed_rows(): lax.all_to_all(own.astype(jnp.bfloat16), far, 0, 0, tiled=True)  32.5 us
    all_to_all x1, waiting for transfers between devices, from_everyone(): return lax.all_to_all(copies, axis, split_axis=0, concat_axis=0, tiled=True)  18.7 us
    all_to_all x1, blocking collectives, from_everyone(): return lax.all_to_all(copies, axis, split_axis=0, concat_axis=0, tiled=True)  8.12 us
    all_to_all x1, blocking collectives, sent_and_summed(): blocks = lax.all_to_all(split_up(x, dim, devices), axis, 0, 0, tiled=True)  6.15 us
    another operation x2, local copies, waits for them, and re-layouts, split_up(): return jnp.moveaxis(x.reshape(*before, devices, -1, *after), dim, 0)  4.74 us
    all_to_all x1, starting transfers between devices, from_everyone(): return lax.all_to_all(copies, axis, split_axis=0, concat_axis=0, tiled=True)  4.3 us
    dot_general x1, matrix products, term_maker(): lax.dot_general(columns, received, (((0,), (0,)), ((), ())), preferred_el...  3.82 us
  transfers between devices with their start and end apart: 2, of which 2 were waited for; matrix products, arithmetic and copies ran while one was open for 1% of the time, Pallas kernels for 0%

commit v1 on v0

v1 whole, which is shorter than its diff:
```python
import jax
import jax.numpy as jnp
from jax import lax
from jax.sharding import Mesh
from jax.sharding import PartitionSpec as P

STEP = 20
DP = ("z", "y", "c")
AXES = ("section", "z", "y", "c")
NZ, NY, NC = 4, 4, 2


def permute(value, sections, route):
    pairs = []
    for s in range(sections):
        for z in range(NZ):
            for y in range(NY):
                for c in range(NC):
                    to = route(s, z, y, c)
                    if to is not None:
                        flat = [((a * NZ + b) * NY + d) * NC + e for a, b, d, e in ((s, z, y, c), to)]
                        pairs.append(tuple(flat))
    return lax.ppermute(value, AXES, pairs)


def slot_rows(rows):
    pair = rows // (NZ * NY * NC)
    slot = lax.broadcasted_iota(jnp.int32, (rows, rows), 0)
    row = lax.broadcasted_iota(jnp.int32, (rows, rows), 1)
    low = slot % pair
    zk = (slot // pair) % NZ
    yj = (slot // (pair * NZ)) % NY
    cx = slot // (pair * NZ * NY)
    far = jnp.where(zk == 0, 2, jnp.where(zk == 1, 1, jnp.where(zk == 2, 3, 0)))
    z = lax.axis_index("z") ^ far
    y = (lax.axis_index("y") + yj) % NY
    c = lax.axis_index("c") ^ 1 ^ cx
    return (row == ((z * NY + y) * NC + c) * pair + low).astype(jnp.bfloat16)


def layer_back(ln_input, ln_grad, top_grad, ln_gain):
    values = ln_input.astype(jnp.float32)
    row_mean = jnp.mean(values, axis=-1, keepdims=True)
    centred = values - row_mean
    inv_std = 1.0 / jnp.sqrt(jnp.mean(centred * centred, axis=-1, keepdims=True) + 1e-05)
    normed = centred * inv_std
    scaled = ln_grad.astype(jnp.float32) * ln_gain[:, None, :]
    inner = (
        scaled
        - jnp.mean(scaled, axis=-1, keepdims=True)
        - normed * jnp.mean(scaled * normed, axis=-1, keepdims=True)
    )
    return (top_grad.astype(jnp.float32) + inner * inv_std).astype(jnp.bfloat16)


def adam_update(grad, master, moment, second):
    new_moment = 0.9 * moment + 0.1 * grad
    new_second = 0.95 * second + 0.05 * grad * grad
    first_fix = 1.0 - 0.9**STEP
    second_fix = 1.0 - 0.95**STEP
    update = new_moment / first_fix / (jnp.sqrt(new_second / second_fix) + 1e-08)
    new_master = master - 0.05 * (update + 0.1 * master)
    return (new_master, new_moment, new_second)


def f32(x):
    return x.astype(jnp.float32)


def b16(x):
    return x.astype(jnp.bfloat16)


def half_reduced(term, sections, only):
    def inside(route):
        return lambda s, z, y, c: route(s, z, y, c) if only is None or s in only else None

    rows = term.shape[0]
    half, chunk = rows // NC, rows // (NC * NY)
    got = permute(b16(term[:half]), sections, inside(lambda s, z, y, c: (s, z, y, 1 - c)))
    chip = term[half:] + f32(got)
    parts = [
        permute(b16(chip[j * chunk : (j + 1) * chunk]), sections, inside(lambda s, z, y, c, j=j: (s, z, (y + j) % NY, c)))
        for j in (2, 1, 3)
    ]
    line = chip[:chunk] + f32(parts[0]) + f32(parts[1]) + f32(parts[2])
    got = permute(b16(line[: chunk // 2]), sections, inside(lambda s, z, y, c: (s, z ^ 1, y, c)))
    return line[chunk // 2 :] + f32(got)


def shards(ln_input, ln_grad, top_grad, ln_gain, hidden, master, moment, second):
    sections = lax.axis_size("section")
    last = sections - 1
    is_last = lax.axis_index("section") == last
    rows, width = hidden.shape[2], master.shape[2]
    own = master.shape[1]
    order = slot_rows(rows)
    own_cols = hidden[0].T
    above = permute(own_cols, sections, lambda s, z, y, c: (s + 1, z, y, c) if s < last else None)

    def term_of(cols, received):
        cols = b16(jnp.dot(order, cols, preferred_element_type=jnp.float32))
        return jnp.dot(cols, received, preferred_element_type=jnp.float32)

    term_last = lax.cond(
        is_last, lambda: term_of(own_cols, top_grad[0]), lambda: jnp.zeros((rows, width), jnp.float32)
    )
    four_last = half_reduced(term_last, sections, (last,))
    got_last = permute(
        b16(four_last[:own]), sections, lambda s, z, y, c: (s, z ^ 3, y, c) if s == last else None
    )
    passed = layer_back(ln_input, ln_grad, top_grad, ln_gain)
    four = half_reduced(term_of(above, passed[0]), sections, None)
    near = permute(b16(four[own:]), sections, lambda s, z, y, c: (s - 1, z, y, c) if s > 0 else None)
    far = permute(b16(four[:own]), sections, lambda s, z, y, c: (s - 1, z ^ 3, y, c) if s > 0 else None)
    grad = jnp.where(is_last, four_last[own:] + f32(got_last), f32(near) + f32(far))
    new_master, new_moment, new_second = adam_update(grad, master[0], moment[0], second[0])
    piece = b16(new_master)
    piece = jnp.concatenate([permute(piece, sections, lambda s, z, y, c: (s, z ^ 3, y, c)), piece])
    piece = jnp.concatenate([permute(piece, sections, lambda s, z, y, c: (s, z ^ 1, y, c)), piece])
    pieces = {
        j: permute(piece, sections, lambda s, z, y, c, j=j: (s, z, (y - j) % NY, c)) for j in (2, 1, 3)
    }
    half = jnp.concatenate([piece, pieces[1], pieces[2], pieces[3]])
    other = permute(half, sections, lambda s, z, y, c: (s, z, y, 1 - c))
    weights = lax.dot_general(
        order, jnp.concatenate([other, half]), (((0,), (0,)), ((), ())), preferred_element_type=jnp.float32
    )
    return (new_master[None], new_moment[None], new_second[None], b16(weights)[None])


def solution(mesh):
    finer = Mesh(mesh.devices.reshape(mesh.shape["section"], NZ, NY, NC), AXES)
    tokens = P("section", DP, None)
    return jax.shard_map(
        shards,
        mesh=finer,
        in_specs=(tokens, tokens, tokens, P("section", None), tokens, tokens, tokens, tokens),
        out_specs=(tokens, tokens, tokens, P("section", None, None)),
        check_vma=False,
    )
```

time: 175 us -> 100 us (0.57); the launches traced: 172 us -> 99.8 us
  waiting for transfers between devices: 87.7 us -> 29.4 us
  blocking collectives: 46.8 us -> 0 us
  starting transfers between devices: 6.46 us -> 44.4 us
  other arithmetic: 15.7 us -> 8.24 us
  matrix products: 3.82 us -> 9.32 us
  local copies, waits for them, and re-layouts: 10.9 us -> 7.48 us
    all_to_all x3 -> x0, blocking collectives: 46.8 us -> none  [the longest x1 32.5 us: summed_rows(): lax.all_to_all(own.astype(jnp.bfloat16), far, 0, 0, tiled=True)]
    ppermute x1 -> x20, starting transfers between devices: 2.15 us -> 44.4 us  [permute(): return lax.ppermute(value, AXES, pairs)]
    ppermute x1 -> x20, waiting for transfers between devices: 69 us -> 29.4 us  [permute(): return lax.ppermute(value, AXES, pairs)]
    all_to_all x1 -> x0, waiting for transfers between devices: 18.7 us -> none  [from_everyone(): return lax.all_to_all(copies, axis, split_axis=0, concat_axis=0, tiled=True)]
    dot_general x1 -> x2, matrix products: 3.82 us -> 9.32 us  [the longest x1 7.4 us: term_of(): return jnp.dot(cols, received, preferred_element_type=jnp.float32)]
    all_to_all x1 -> x0, starting transfers between devices: 4.3 us -> none  [from_everyone(): return lax.all_to_all(copies, axis, split_axis=0, concat_axis=0, tiled=True)]
    another operation x3 -> x1, local copies, waits for them, and re-layouts: 6.24 us -> 1.94 us  [the longest x2 4.74 us: split_up(): return jnp.moveaxis(x.reshape(*before, devices, -1, *after), dim, 0)]
    slice x0 -> x8, local copies, waits for them, and re-layouts: none -> 4.22 us  [the longest x2 3.97 us: half_reduced(): term[:half]]
  transfers between devices with their start and end apart: 2 -> 20, of which waited for: 2 -> 10; matrix products, arithmetic and copies ran while one was open for 1% -> 20% of each run, Pallas kernels for 0% -> 0%
where the time goes in v1:
time: 100 us; the launch traced here: 99.8 us
  starting transfers between devices  44.4 us (44%)
  waiting for transfers between devices  29.4 us (29%)
  matrix products  9.32 us (9%)
  other arithmetic  8.24 us (8%)
  local copies, waits for them, and re-layouts  7.48 us (7%)
    ppermute x20, starting transfers between devices, permute(): return lax.ppermute(value, AXES, pairs)  44.4 us
    ppermute x20, waiting for transfers between devices, permute(): return lax.ppermute(value, AXES, pairs)  29.4 us
    dot_general x1, matrix products, term_of(): return jnp.dot(cols, received, preferred_element_type=jnp.float32)  7.4 us
    slice x2, local copies, waits for them, and re-layouts, half_reduced(): term[:half]  3.97 us
    reduce_sum x1, other arithmetic, layer_back(): jnp.mean(scaled, axis=-1, keepdims=True)  2.08 us
    another operation x3, other arithmetic  2.04 us
  transfers between devices with their start and end apart: 20, of which 10 were waited for; matrix products, arithmetic and copies ran while one was open for 20% of the time, Pallas kernels for 0%

profile of v1, /device:TPU:37, one launch (start us, length us, event | category | flops | bytes accessed | tf_op | source)
XLA Modules:
  0.0 99.8 jit_solution(7305875335066092899)
XLA Ops:
  0.6 2.8 %collective-permute-start.6 = (bf16[64,128]{1,0:T(8,128)(2,1)}, bf16[64,128]{1,0:T(8,128)(2,1)S(1)}, u32[]{:S(2)}, u32[]{:S(2)}) collective-permute-start(bf16[64,128]{1,0:T(8,128)(2,1)} %bitcast.48), channel_id=1, source_target_pairs={{0,32},{1,33},{2,34},{3,35},{4,36},{5,37},{6,38},{7,39},{8,40},{9,... | collective-permute-start | bytes 49160 | tf_op jit(solution)/shard_map/ppermute | solution.py:23
  3.6 0.2 fusion.42
  3.7 0.0 copy-start
  3.7 2.0 %conditional.1 = (f32[64,12288]{1,0:T(8,128)}) conditional(s32[]{:T(128)} %convert_element_type.82, () %tuple.14, (bf16[64,64]{1,0:T(8,128)(2,1)S(1)}, bf16[64,128]{1,0:T(8,128)(2,1)}, bf16[1,128,12288]{2,1,0:T(8,128)(2,1)}) %tuple.37), branch_computations={%region_0.1_spmd, %region_1.2_spmd} | conditional | flops 202383360 | bytes 6316040 | solution.py:105
  3.8 1.9 %broadcast.136 = f32[64,12288]{1,0:T(8,128)} broadcast(f32[]{:T(128)} %constant.106.clone), dimensions={} | broadcast | bytes 3145732 | tf_op jit(solution)/shard_map/broadcast.7
  5.7 2.5 %slice.138 = bf16[32,12288]{1,0:T(8,128)(2,1)} slice(f32[64,12288]{1,0:T(8,128)} %get-tuple-element.49), slice={[0:32], [0:12288]} | slice | bytes 1572864 | tf_op jit(solution)/shard_map/slice | solution.py:80
  8.2 1.7 %collective-permute-start = (bf16[32,12288]{1,0:T(8,128)(2,1)}, bf16[32,12288]{1,0:T(8,128)(2,1)}, u32[]{:S(2)}, u32[]{:S(2)}) collective-permute-start(bf16[32,12288]{1,0:T(8,128)(2,1)} %slice.138), channel_id=1, source_target_pairs={{224,225},{225,224},{226,227},{227,226},{228,229},{229,228},{230,2... | collective-permute-start | bytes 2359304 | tf_op jit(solution)/shard_map/ppermute | solution.py:23
  9.9 0.5 convert_reduce_fusion
  10.4 1.0 %fusion.12 = f32[128]{0:T(128)S(1)} fusion(bf16[1,128,12288]{2,1,0:T(8,128)(2,1)S(1)} %copy-done, f32[128]{0:T(128)S(1)} %broadcast_multiply_fusion.1), kind=kLoop, calls=%fused_computation.16 | loop fusion | flops 6291328 | bytes 3146752 | tf_op jit(solution)/shard_map/reduce_sum | solution.py:45
  11.4 2.1 %fusion.13 = (f32[128]{0:T(128)S(1)}, f32[128]{0:T(128)S(1)}) fusion(bf16[1,128,12288]{2,1,0:T(8,128)(2,1)S(1)} %copy-done.1, f32[12288]{0:T(1024)S(1)} %bitcast.46, f32[128]{0:T(128)S(1)} %add_rsqrt_fusion, f32[128]{0:T(128)S(1)} %broadcast_multiply_fusion.1, bf16[1,128,12288]{2,1,0:T(8,128)(2,1)S(1)} %copy-done), kind=kLoop, calls=%fused_computation.18 | loop fusion | flops 12582656 | bytes 6342656 | tf_op jit(solution)/shard_map/reduce_sum | solution.py:50
  13.5 0.0 collective-permute-done.6
  13.5 7.4 %fusion.15 = f32[64,12288]{1,0:T(8,128)} fusion(bf16[1,128,12288]{2,1,0:T(8,128)(2,1)S(1)} %copy-done, bf16[1,128,12288]{2,1,0:T(8,128)(2,1)} %param.11, bf16[1,128,12288]{2,1,0:T(8,128)(2,1)} %param.12, f32[128]{0:T(128)S(1)} %get-tuple-element.35, f32[128]{0:T(128)S(1)} %add_rsqrt_fusion, f32[128]{0:T(128)S(1)} %broadcast_multiply_fusion.1, ...), kind=kOutput, calls=%fused_computation.20 | convolution fusion | flops 221474816 | bytes 12652812 | tf_op jit(solution)/shard_map/dot_general | solution.py:103
  20.9 1.5 %slice.137 = bf16[32,12288]{1,0:T(8,128)(2,1)S(1)} slice(f32[64,12288]{1,0:T(8,128)} %fusion.15), slice={[0:32], [0:12288]} | slice | bytes 1572864 | tf_op jit(solution)/shard_map/slice | solution.py:80
  22.4 1.0 %collective-permute-start.7 = (bf16[32,12288]{1,0:T(8,128)(2,1)S(1)}, bf16[32,12288]{1,0:T(8,128)(2,1)S(1)}, u32[]{:S(2)}, u32[]{:S(2)}) collective-permute-start(bf16[32,12288]{1,0:T(8,128)(2,1)S(1)} %slice.137), channel_id=1, source_target_pairs={{0,1},{1,0},{2,3},{3,2},{4,5},{5,4},{6,7},{7,6},{8,9},{9,8},{10,11... | collective-permute-start | bytes 2359304 | tf_op jit(solution)/shard_map/ppermute | solution.py:23
  23.4 0.0 collective-permute-done
  23.4 1.8 %fusion.46 = (bf16[32,12288]{1,0:T(8,128)(2,1)S(1)}, f32[32,12288]{1,0:T(8,128)S(1)}) fusion(bf16[32,12288]{1,0:T(8,128)(2,1)} %collective-permute-done, f32[64,12288]{1,0:T(8,128)} %get-tuple-element.49), kind=kLoop, calls=%fused_computation.97 | loop fusion | flops 1179648 | bytes 4718592 | tf_op jit(solution)/shard_map/convert.11
  25.3 0.7 collective-permute-start.1
  26.0 0.7 collective-permute-start.3
  26.7 0.7 collective-permute-start.2
  27.4 0.0 collective-permute-done.7
  27.4 0.2 fusion.45
  27.5 0.0 copy-start.3
  27.6 0.0 copy-start.4
  27.6 0.0 copy-start.5
  27.6 3.0 %collective-permute-start.8 = (bf16[8,12288]{1,0:T(8,128)(2,1)S(1)}, bf16[8,12288]{1,0:T(8,128)(2,1)S(1)}, u32[]{:S(2)}, u32[]{:S(2)}) collective-permute-start(bf16[8,12288]{1,0:T(8,128)(2,1)S(1)} %get-tuple-element.28), channel_id=1, source_target_pairs={{0,4},{1,5},{2,6},{3,7},{4,0},{5,1},{6,2},{7,3},{8,12},{9,13},{10,... | collective-permute-start | bytes 589832 | tf_op jit(solution)/shard_map/ppermute | solution.py:23
  30.6 0.8 collective-permute-start.10
  31.4 0.7 collective-permute-start.9
  32.1 0.0 collective-permute-done.2
  32.1 0.1 fusion.20
  32.2 0.7 collective-permute-start.4
  32.9 2.6 %collective-permute-done.8 = bf16[8,12288]{1,0:T(8,128)(2,1)S(1)} collective-permute-done((bf16[8,12288]{1,0:T(8,128)(2,1)S(1)}, bf16[8,12288]{1,0:T(8,128)(2,1)S(1)}, u32[]{:S(2)}, u32[]{:S(2)}) %collective-permute-start.8) | collective-permute-done | bytes 196640 | tf_op jit(solution)/shard_map/ppermute | solution.py:23
  35.5 4.6 %collective-permute-done.10 = bf16[8,12288]{1,0:T(8,128)(2,1)S(1)} collective-permute-done((bf16[8,12288]{1,0:T(8,128)(2,1)S(1)}, bf16[8,12288]{1,0:T(8,128)(2,1)S(1)}, u32[]{:S(2)}, u32[]{:S(2)}) %collective-permute-start.10) | collective-permute-done | bytes 196640 | tf_op jit(solution)/shard_map/ppermute | solution.py:23
  40.1 0.0 collective-permute-done.9
  40.1 0.1 fusion.18
  40.2 3.1 %collective-permute-start.11 = (bf16[4,12288]{1,0:T(4,128)(2,1)S(1)}, bf16[4,12288]{1,0:T(4,128)(2,1)S(1)}, u32[]{:S(2)}, u32[]{:S(2)}) collective-permute-start(bf16[4,12288]{1,0:T(4,128)(2,1)S(1)} %slice.139), channel_id=1, source_target_pairs={{0,8},{1,9},{2,10},{3,11},{4,12},{5,13},{6,14},{7,15},{8,0},{9,1},... | collective-permute-start | bytes 294920 | tf_op jit(solution)/shard_map/ppermute | solution.py:23
  43.3 0.0 collective-permute-done.4
  43.3 0.1 slice_add_fusion.5
  43.4 0.8 collective-permute-start.5
  44.3 2.9 %collective-permute-done.11 = bf16[4,12288]{1,0:T(4,128)(2,1)S(1)} collective-permute-done((bf16[4,12288]{1,0:T(4,128)(2,1)S(1)}, bf16[4,12288]{1,0:T(4,128)(2,1)S(1)}, u32[]{:S(2)}, u32[]{:S(2)}) %collective-permute-start.11) | collective-permute-done | bytes 98336 | tf_op jit(solution)/shard_map/ppermute | solution.py:23
  47.2 0.1 fusion.21
  47.2 0.1 fusion.49
  47.3 2.5 %collective-permute-start.12 = (bf16[2,12288]{1,0:T(2,128)(2,1)S(1)}, bf16[2,12288]{1,0:T(2,128)(2,1)S(1)}, u32[]{:S(2)}, u32[]{:S(2)}) collective-permute-start(bf16[2,12288]{1,0:T(2,128)(2,1)S(1)} %get-tuple-element.33), channel_id=1, source_target_pairs={{32,0},{33,1},{34,2},{35,3},{36,4},{37,5},{38,6},{39,7},{40,8},{41... | collective-permute-start | bytes 147464 | tf_op jit(solution)/shard_map/ppermute | solution.py:23
  49.8 7.4 %collective-permute-start.13 = (bf16[2,12288]{1,0:T(2,128)(2,1)S(1)}, bf16[2,12288]{1,0:T(2,128)(2,1)S(1)}, u32[]{:S(2)}, u32[]{:S(2)}) collective-permute-start(bf16[2,12288]{1,0:T(2,128)(2,1)S(1)} %get-tuple-element.34), channel_id=1, source_target_pairs={{32,24},{33,25},{34,26},{35,27},{36,28},{37,29},{38,30},{39,31},{4... | collective-permute-start | bytes 147464 | tf_op jit(solution)/shard_map/ppermute | solution.py:23
  57.2 6.3 %collective-permute-done.12 = bf16[2,12288]{1,0:T(2,128)(2,1)S(1)} collective-permute-done((bf16[2,12288]{1,0:T(2,128)(2,1)S(1)}, bf16[2,12288]{1,0:T(2,128)(2,1)S(1)}, u32[]{:S(2)}, u32[]{:S(2)}) %collective-permute-start.12) | collective-permute-done | bytes 49184 | tf_op jit(solution)/shard_map/ppermute | solution.py:23
  63.6 2.0 %collective-permute-done.13 = bf16[2,12288]{1,0:T(2,128)(2,1)S(1)} collective-permute-done((bf16[2,12288]{1,0:T(2,128)(2,1)S(1)}, bf16[2,12288]{1,0:T(2,128)(2,1)S(1)}, u32[]{:S(2)}, u32[]{:S(2)}) %collective-permute-start.13) | collective-permute-done | bytes 49184 | tf_op jit(solution)/shard_map/ppermute | solution.py:23
  65.6 1.1 %fusion.43 = (bf16[2,12288]{1,0:T(2,128)(2,1)S(1)}, f32[2,12288]{1,0:T(2,128)}, f32[2,12288]{1,0:T(2,128)S(1)}) fusion(f32[1,2,12288]{2,1,0:T(2,128)S(1)} %copy-done.3, f32[1,2,12288]{2,1,0:T(2,128)S(1)} %copy-done.4, f32[1,2,12288]{2,1,0:T(2,128)S(1)} %copy-done.5, bf16[2,12288]{1,0:T(2,128)(2,1)S(1)} %collective-permute-done.13, ...), kind=kLoop, calls=%fused_computation.95 | loop fusion | flops 540672 | bytes 786433 | tf_op jit(solution)/shard_map/convert_element_type | solution.py:71
  66.7 2.6 %collective-permute-start.14 = (bf16[2,12288]{1,0:T(2,128)(2,1)S(1)}, bf16[2,12288]{1,0:T(2,128)(2,1)S(1)}, u32[]{:S(2)}, u32[]{:S(2)}) collective-permute-start(bf16[2,12288]{1,0:T(2,128)(2,1)S(1)} %get-tuple-element.18), channel_id=1, source_target_pairs={{0,24},{1,25},{2,26},{3,27},{4,28},{5,29},{6,30},{7,31},{8,16},{9,... | collective-permute-start | bytes 147464 | tf_op jit(solution)/shard_map/ppermute | solution.py:23
  69.3 2.5 %collective-permute-done.14 = bf16[2,12288]{1,0:T(2,128)(2,1)S(1)} collective-permute-done((bf16[2,12288]{1,0:T(2,128)(2,1)S(1)}, bf16[2,12288]{1,0:T(2,128)(2,1)S(1)}, u32[]{:S(2)}, u32[]{:S(2)}) %collective-permute-start.14) | collective-permute-done | bytes 49184 | tf_op jit(solution)/shard_map/ppermute | solution.py:23
  71.7 0.1 pad_maximum_fusion.1
  71.9 2.3 %collective-permute-start.15 = (bf16[4,12288]{1,0:T(4,128)(2,1)S(1)}, bf16[4,12288]{1,0:T(4,128)(2,1)S(1)}, u32[]{:S(2)}, u32[]{:S(2)}) collective-permute-start(bf16[4,12288]{1,0:T(4,128)(2,1)S(1)} %pad_maximum_fusion.1), channel_id=1, source_target_pairs={{0,8},{1,9},{2,10},{3,11},{4,12},{5,13},{6,14},{7,15},{8,0},{9,1},... | collective-permute-start | bytes 294920 | tf_op jit(solution)/shard_map/ppermute | solution.py:23
  74.1 2.2 %collective-permute-done.15 = bf16[4,12288]{1,0:T(4,128)(2,1)S(1)} collective-permute-done((bf16[4,12288]{1,0:T(4,128)(2,1)S(1)}, bf16[4,12288]{1,0:T(4,128)(2,1)S(1)}, u32[]{:S(2)}, u32[]{:S(2)}) %collective-permute-start.15) | collective-permute-done | bytes 98336 | tf_op jit(solution)/shard_map/ppermute | solution.py:23
  76.3 0.2 pad_maximum_fusion
  76.5 0.1 collective-permute-start.18
  76.6 3.4 %collective-permute-start.17 = (bf16[8,12288]{1,0:T(8,128)(2,1)S(1)}, bf16[8,12288]{1,0:T(8,128)(2,1)S(1)}, u32[]{:S(2)}, u32[]{:S(2)}) collective-permute-start(bf16[8,12288]{1,0:T(8,128)(2,1)S(1)} %pad_maximum_fusion), channel_id=1, source_target_pairs={{0,4},{1,5},{2,6},{3,7},{4,0},{5,1},{6,2},{7,3},{8,12},{9,13},{10,... | collective-permute-start | bytes 589832 | tf_op jit(solution)/shard_map/ppermute | solution.py:23
  79.9 0.0 collective-permute-start.16
  79.9 2.3 %collective-permute-done.18 = bf16[8,12288]{1,0:T(8,128)(2,1)S(1)} collective-permute-done((bf16[8,12288]{1,0:T(8,128)(2,1)S(1)}, bf16[8,12288]{1,0:T(8,128)(2,1)S(1)}, u32[]{:S(2)}, u32[]{:S(2)}) %collective-permute-start.18) | collective-permute-done | bytes 196640 | tf_op jit(solution)/shard_map/ppermute | solution.py:23
  82.3 2.8 %collective-permute-done.17 = bf16[8,12288]{1,0:T(8,128)(2,1)S(1)} collective-permute-done((bf16[8,12288]{1,0:T(8,128)(2,1)S(1)}, bf16[8,12288]{1,0:T(8,128)(2,1)S(1)}, u32[]{:S(2)}, u32[]{:S(2)}) %collective-permute-start.17) | collective-permute-done | bytes 196640 | tf_op jit(solution)/shard_map/ppermute | solution.py:23
  85.1 0.0 collective-permute-done.16
  85.1 0.5 concatenate.17
  85.6 9.6 %collective-permute-start.19 = (bf16[32,12288]{1,0:T(8,128)(2,1)S(1)}, bf16[32,12288]{1,0:T(8,128)(2,1)S(1)}, u32[]{:S(2)}, u32[]{:S(2)}) collective-permute-start(bf16[32,12288]{1,0:T(8,128)(2,1)S(1)} %concatenate.17), channel_id=1, source_target_pairs={{0,1},{1,0},{2,3},{3,2},{4,5},{5,4},{6,7},{7,6},{8,9},{9,8},{10,11... | collective-permute-start | bytes 2359304 | tf_op jit(solution)/shard_map/ppermute | solution.py:23
  95.2 0.8 fusion.38
  96.1 1.1 %collective-permute-done.19 = bf16[32,12288]{1,0:T(8,128)(2,1)S(1)} collective-permute-done((bf16[32,12288]{1,0:T(8,128)(2,1)S(1)}, bf16[32,12288]{1,0:T(8,128)(2,1)S(1)}, u32[]{:S(2)}, u32[]{:S(2)}) %collective-permute-start.19) | collective-permute-done | bytes 786464 | tf_op jit(solution)/shard_map/ppermute | solution.py:23
  97.1 0.8 concatenate.18
  97.9 1.9 %fusion.2 = bf16[1,64,12288]{2,1,0:T(8,128)(2,1)} fusion(bf16[64,12288]{1,0:T(8,128)(2,1)S(1)} %concatenate.18, s32[64]{0:T(128)S(1)} %get-tuple-element.42, s32[64]{0:T(128)S(1)} %get-tuple-element.45, s32[64]{0:T(128)S(1)} %get-tuple-element.43, s32[64]{0:T(128)S(1)} %get-tuple-element.46, s32[]{:T(128)S(6)} %xor.17, s32[64]{0:T(128)S(1)} %get-tuple-element.44, ...), kind=kOutput, calls=%fused_computation.4 | convolution fusion | flops 101666816 | bytes 3148044 | tf_op jit(solution)/shard_map/dot_general | solution.py:126
  (27 shorter events, 0.3 us)
Async XLA Ops:
  0.6 12.9 %collective-permute-start.6 = (bf16[64,128]{1,0:T(8,128)(2,1)}, bf16[64,128]{1,0:T(8,128)(2,1)S(1)}, u32[]{:S(2)}, u32[]{:S(2)}) collective-permute-start(bf16[64,128]{1,0:T(8,128)(2,1)} %bitcast.48), channel_id=1, source_target_pairs={{0,32},{1,33},{2,34},{3,35},{4,36},{5,37},{6,38},{7,39},{8,40},{9,... | collective-permute-start | bytes 49160 | tf_op jit(solution)/shard_map/ppermute | solution.py:23
  3.7 6.1 %copy-start = (bf16[1,128,12288]{2,1,0:T(8,128)(2,1)S(1)}, bf16[1,128,12288]{2,1,0:T(8,128)(2,1)}, u32[]{:S(2)}) copy-start(bf16[1,128,12288]{2,1,0:T(8,128)(2,1)} %param.10) | copy-start | bytes 9437188
  8.2 3.2 %copy-start.1 = (bf16[1,128,12288]{2,1,0:T(8,128)(2,1)S(1)}, bf16[1,128,12288]{2,1,0:T(8,128)(2,1)}, u32[]{:S(2)}) copy-start(bf16[1,128,12288]{2,1,0:T(8,128)(2,1)} %param.11) | copy-start | bytes 9437188
  8.2 3.2 %copy-start.6 = (f32[1,12288]{1,0:T(1,128)S(1)}, f32[1,12288]{1,0:T(1,128)}, u32[]{:S(2)}) copy-start(f32[1,12288]{1,0:T(1,128)} %param.13) | copy-start | bytes 147460
  8.2 15.3 %collective-permute-start = (bf16[32,12288]{1,0:T(8,128)(2,1)}, bf16[32,12288]{1,0:T(8,128)(2,1)}, u32[]{:S(2)}, u32[]{:S(2)}) collective-permute-start(bf16[32,12288]{1,0:T(8,128)(2,1)} %slice.138), channel_id=1, source_target_pairs={{224,225},{225,224},{226,227},{227,226},{228,229},{229,228},{230,2... | collective-permute-start | bytes 2359304 | tf_op jit(solution)/shard_map/ppermute | solution.py:23
  22.4 5.0 %copy-start.2 = (f32[64,12288]{1,0:T(8,128)S(1)}, f32[64,12288]{1,0:T(8,128)}, u32[]{:S(2)}) copy-start(f32[64,12288]{1,0:T(8,128)} %fusion.15) | copy-start | bytes 9437188
  22.4 5.0 %collective-permute-start.7 = (bf16[32,12288]{1,0:T(8,128)(2,1)S(1)}, bf16[32,12288]{1,0:T(8,128)(2,1)S(1)}, u32[]{:S(2)}, u32[]{:S(2)}) collective-permute-start(bf16[32,12288]{1,0:T(8,128)(2,1)S(1)} %slice.137), channel_id=1, source_target_pairs={{0,1},{1,0},{2,3},{3,2},{4,5},{5,4},{6,7},{7,6},{8,9},{9,8},{10,11... | collective-permute-start | bytes 2359304 | tf_op jit(solution)/shard_map/ppermute | solution.py:23
  25.3 6.1 %collective-permute-start.1 = (bf16[8,12288]{1,0:T(8,128)(2,1)S(1)}, bf16[8,12288]{1,0:T(8,128)(2,1)S(1)}, u32[]{:S(2)}, u32[]{:S(2)}) collective-permute-start(bf16[8,12288]{1,0:T(8,128)(2,1)S(1)} %get-tuple-element.25), channel_id=1, source_target_pairs={{224,228},{225,229},{226,230},{227,231},{228,224},{229,225},{230,2... | collective-permute-start | bytes 589832 | tf_op jit(solution)/shard_map/ppermute | solution.py:23
  26.0 6.1 %collective-permute-start.3 = (bf16[8,12288]{1,0:T(8,128)(2,1)S(1)}, bf16[8,12288]{1,0:T(8,128)(2,1)S(1)}, u32[]{:S(2)}, u32[]{:S(2)}) collective-permute-start(bf16[8,12288]{1,0:T(8,128)(2,1)S(1)} %get-tuple-element.26), channel_id=1, source_target_pairs={{224,230},{225,231},{226,224},{227,225},{228,226},{229,227},{230,2... | collective-permute-start | bytes 589832 | tf_op jit(solution)/shard_map/ppermute | solution.py:23
  26.7 5.4 %collective-permute-start.2 = (bf16[8,12288]{1,0:T(8,128)(2,1)S(1)}, bf16[8,12288]{1,0:T(8,128)(2,1)S(1)}, u32[]{:S(2)}, u32[]{:S(2)}) collective-permute-start(bf16[8,12288]{1,0:T(8,128)(2,1)S(1)} %get-tuple-element.27), channel_id=1, source_target_pairs={{224,226},{225,227},{226,228},{227,229},{228,230},{229,231},{230,2... | collective-permute-start | bytes 589832 | tf_op jit(solution)/shard_map/ppermute | solution.py:23
  27.5 38.1 %copy-start.3 = (f32[1,2,12288]{2,1,0:T(2,128)S(1)}, f32[1,2,12288]{2,1,0:T(2,128)}, u32[]{:S(2)}) copy-start(f32[1,2,12288]{2,1,0:T(2,128)} %param.17) | copy-start | bytes 294916
  27.6 38.1 %copy-start.4 = (f32[1,2,12288]{2,1,0:T(2,128)S(1)}, f32[1,2,12288]{2,1,0:T(2,128)}, u32[]{:S(2)}) copy-start(f32[1,2,12288]{2,1,0:T(2,128)} %param.16) | copy-start | bytes 294916
  27.6 38.0 %copy-start.5 = (f32[1,2,12288]{2,1,0:T(2,128)S(1)}, f32[1,2,12288]{2,1,0:T(2,128)}, u32[]{:S(2)}) copy-start(f32[1,2,12288]{2,1,0:T(2,128)} %param.15) | copy-start | bytes 294916
  27.6 7.9 %collective-permute-start.8 = (bf16[8,12288]{1,0:T(8,128)(2,1)S(1)}, bf16[8,12288]{1,0:T(8,128)(2,1)S(1)}, u32[]{:S(2)}, u32[]{:S(2)}) collective-permute-start(bf16[8,12288]{1,0:T(8,128)(2,1)S(1)} %get-tuple-element.28), channel_id=1, source_target_pairs={{0,4},{1,5},{2,6},{3,7},{4,0},{5,1},{6,2},{7,3},{8,12},{9,13},{10,... | collective-permute-start | bytes 589832 | tf_op jit(solution)/shard_map/ppermute | solution.py:23
  30.6 9.5 %collective-permute-start.10 = (bf16[8,12288]{1,0:T(8,128)(2,1)S(1)}, bf16[8,12288]{1,0:T(8,128)(2,1)S(1)}, u32[]{:S(2)}, u32[]{:S(2)}) collective-permute-start(bf16[8,12288]{1,0:T(8,128)(2,1)S(1)} %get-tuple-element.29), channel_id=1, source_target_pairs={{0,6},{1,7},{2,0},{3,1},{4,2},{5,3},{6,4},{7,5},{8,14},{9,15},{10,... | collective-permute-start | bytes 589832 | tf_op jit(solution)/shard_map/ppermute | solution.py:23
  31.4 8.7 %collective-permute-start.9 = (bf16[8,12288]{1,0:T(8,128)(2,1)S(1)}, bf16[8,12288]{1,0:T(8,128)(2,1)S(1)}, u32[]{:S(2)}, u32[]{:S(2)}) collective-permute-start(bf16[8,12288]{1,0:T(8,128)(2,1)S(1)} %get-tuple-element.30), channel_id=1, source_target_pairs={{0,2},{1,3},{2,4},{3,5},{4,6},{5,7},{6,0},{7,1},{8,10},{9,11},{10,... | collective-permute-start | bytes 589832 | tf_op jit(solution)/shard_map/ppermute | solution.py:23
  32.2 11.1 %collective-permute-start.4 = (bf16[4,12288]{1,0:T(4,128)(2,1)S(1)}, bf16[4,12288]{1,0:T(4,128)(2,1)S(1)}, u32[]{:S(2)}, u32[]{:S(2)}) collective-permute-start(bf16[4,12288]{1,0:T(4,128)(2,1)S(1)} %slice.140), channel_id=1, source_target_pairs={{224,232},{225,233},{226,234},{227,235},{228,236},{229,237},{230,2... | collective-permute-start | bytes 294920 | tf_op jit(solution)/shard_map/ppermute | solution.py:23
  40.2 6.9 %collective-permute-start.11 = (bf16[4,12288]{1,0:T(4,128)(2,1)S(1)}, bf16[4,12288]{1,0:T(4,128)(2,1)S(1)}, u32[]{:S(2)}, u32[]{:S(2)}) collective-permute-start(bf16[4,12288]{1,0:T(4,128)(2,1)S(1)} %slice.139), channel_id=1, source_target_pairs={{0,8},{1,9},{2,10},{3,11},{4,12},{5,13},{6,14},{7,15},{8,0},{9,1},... | collective-permute-start | bytes 294920 | tf_op jit(solution)/shard_map/ppermute | solution.py:23
  43.4 13.8 %collective-permute-start.5 = (bf16[2,12288]{1,0:T(2,128)(2,1)S(1)}, bf16[2,12288]{1,0:T(2,128)(2,1)S(1)}, u32[]{:S(2)}, u32[]{:S(2)}) collective-permute-start(bf16[2,12288]{1,0:T(2,128)(2,1)S(1)} %slice.141), channel_id=1, source_target_pairs={{224,248},{225,249},{226,250},{227,251},{228,252},{229,253},{230,2... | collective-permute-start | bytes 147464 | tf_op jit(solution)/shard_map/ppermute | solution.py:23
  47.3 16.3 %collective-permute-start.12 = (bf16[2,12288]{1,0:T(2,128)(2,1)S(1)}, bf16[2,12288]{1,0:T(2,128)(2,1)S(1)}, u32[]{:S(2)}, u32[]{:S(2)}) collective-permute-start(bf16[2,12288]{1,0:T(2,128)(2,1)S(1)} %get-tuple-element.33), channel_id=1, source_target_pairs={{32,0},{33,1},{34,2},{35,3},{36,4},{37,5},{38,6},{39,7},{40,8},{41... | collective-permute-start | bytes 147464 | tf_op jit(solution)/shard_map/ppermute | solution.py:23
  49.8 15.8 %collective-permute-start.13 = (bf16[2,12288]{1,0:T(2,128)(2,1)S(1)}, bf16[2,12288]{1,0:T(2,128)(2,1)S(1)}, u32[]{:S(2)}, u32[]{:S(2)}) collective-permute-start(bf16[2,12288]{1,0:T(2,128)(2,1)S(1)} %get-tuple-element.34), channel_id=1, source_target_pairs={{32,24},{33,25},{34,26},{35,27},{36,28},{37,29},{38,30},{39,31},{4... | collective-permute-start | bytes 147464 | tf_op jit(solution)/shard_map/ppermute | solution.py:23
  66.7 5.0 %collective-permute-start.14 = (bf16[2,12288]{1,0:T(2,128)(2,1)S(1)}, bf16[2,12288]{1,0:T(2,128)(2,1)S(1)}, u32[]{:S(2)}, u32[]{:S(2)}) collective-permute-start(bf16[2,12288]{1,0:T(2,128)(2,1)S(1)} %get-tuple-element.18), channel_id=1, source_target_pairs={{0,24},{1,25},{2,26},{3,27},{4,28},{5,29},{6,30},{7,31},{8,16},{9,... | collective-permute-start | bytes 147464 | tf_op jit(solution)/shard_map/ppermute | solution.py:23
  71.9 4.5 %collective-permute-start.15 = (bf16[4,12288]{1,0:T(4,128)(2,1)S(1)}, bf16[4,12288]{1,0:T(4,128)(2,1)S(1)}, u32[]{:S(2)}, u32[]{:S(2)}) collective-permute-start(bf16[4,12288]{1,0:T(4,128)(2,1)S(1)} %pad_maximum_fusion.1), channel_id=1, source_target_pairs={{0,8},{1,9},{2,10},{3,11},{4,12},{5,13},{6,14},{7,15},{8,0},{9,1},... | collective-permute-start | bytes 294920 | tf_op jit(solution)/shard_map/ppermute | solution.py:23
  76.5 5.8 %collective-permute-start.18 = (bf16[8,12288]{1,0:T(8,128)(2,1)S(1)}, bf16[8,12288]{1,0:T(8,128)(2,1)S(1)}, u32[]{:S(2)}, u32[]{:S(2)}) collective-permute-start(bf16[8,12288]{1,0:T(8,128)(2,1)S(1)} %pad_maximum_fusion), channel_id=1, source_target_pairs={{0,2},{1,3},{2,4},{3,5},{4,6},{5,7},{6,0},{7,1},{8,10},{9,11},{10,... | collective-permute-start | bytes 589832 | tf_op jit(solution)/shard_map/ppermute | solution.py:23
  76.6 8.5 %collective-permute-start.17 = (bf16[8,12288]{1,0:T(8,128)(2,1)S(1)}, bf16[8,12288]{1,0:T(8,128)(2,1)S(1)}, u32[]{:S(2)}, u32[]{:S(2)}) collective-permute-start(bf16[8,12288]{1,0:T(8,128)(2,1)S(1)} %pad_maximum_fusion), channel_id=1, source_target_pairs={{0,4},{1,5},{2,6},{3,7},{4,0},{5,1},{6,2},{7,3},{8,12},{9,13},{10,... | collective-permute-start | bytes 589832 | tf_op jit(solution)/shard_map/ppermute | solution.py:23
  79.9 5.2 %collective-permute-start.16 = (bf16[8,12288]{1,0:T(8,128)(2,1)S(1)}, bf16[8,12288]{1,0:T(8,128)(2,1)S(1)}, u32[]{:S(2)}, u32[]{:S(2)}) collective-permute-start(bf16[8,12288]{1,0:T(8,128)(2,1)S(1)} %pad_maximum_fusion), channel_id=1, source_target_pairs={{0,6},{1,7},{2,0},{3,1},{4,2},{5,3},{6,4},{7,5},{8,14},{9,15},{10,... | collective-permute-start | bytes 589832 | tf_op jit(solution)/shard_map/ppermute | solution.py:23
  85.6 11.5 %collective-permute-start.19 = (bf16[32,12288]{1,0:T(8,128)(2,1)S(1)}, bf16[32,12288]{1,0:T(8,128)(2,1)S(1)}, u32[]{:S(2)}, u32[]{:S(2)}) collective-permute-start(bf16[32,12288]{1,0:T(8,128)(2,1)S(1)} %concatenate.17), channel_id=1, source_target_pairs={{0,1},{1,0},{2,3},{3,2},{4,5},{5,4},{6,7},{7,6},{8,9},{9,8},{10,11... | collective-permute-start | bytes 2359304 | tf_op jit(solution)/shard_map/ppermute | solution.py:23

commit v2 on v1

v2 whole, which is shorter than its diff:
```python
import jax
import jax.numpy as jnp
from jax import lax
from jax.experimental import pallas as pl
from jax.experimental.pallas import tpu as pltpu
from jax.sharding import Mesh
from jax.sharding import PartitionSpec as P

STEP = 20
DP = ("z", "y", "c")
AXES = ("section", "z", "y", "c")
NZ, NY, NC = 4, 4, 2
LANES = 128
ROWBLOCK = 32
CHUNK = 1024
FAR = (2, 1, 3, 0)


def permute(value, route):
    sections = lax.axis_size("section")
    pairs = []
    for s in range(sections):
        for z in range(NZ):
            for y in range(NY):
                for c in range(NC):
                    to = route(s, z, y, c)
                    flat = [((a % sections * NZ + b) * NY + d % NY) * NC + e for a, b, d, e in ((s, z, y, c), to)]
                    pairs.append(tuple(flat))
    return lax.ppermute(value, AXES, pairs)


def slot_rows(rows):
    pair = rows // (NZ * NY * NC)
    slot = lax.broadcasted_iota(jnp.int32, (rows, rows), 0)
    row = lax.broadcasted_iota(jnp.int32, (rows, rows), 1)
    low = slot % pair
    zk = (slot // pair) % NZ
    yj = (slot // (pair * NZ)) % NY
    cx = slot // (pair * NZ * NY)
    far = jnp.where(zk == 0, FAR[0], jnp.where(zk == 1, FAR[1], jnp.where(zk == 2, FAR[2], FAR[3])))
    z = lax.axis_index("z") ^ far
    y = (lax.axis_index("y") + yj) % NY
    c = lax.axis_index("c") ^ 1 ^ cx
    return (row == ((z * NY + y) * NC + c) * pair + low).astype(jnp.bfloat16)


def f32(x):
    return x.astype(jnp.float32)


def b16(x):
    return x.astype(jnp.bfloat16)


def adam_update(grad, master, moment, second):
    new_moment = 0.9 * moment + 0.1 * grad
    new_second = 0.95 * second + 0.05 * grad * grad
    first_fix = 1.0 - 0.9**STEP
    second_fix = 1.0 - 0.95**STEP
    update = new_moment / first_fix / (jnp.sqrt(new_second / second_fix) + 1e-08)
    new_master = master - 0.05 * (update + 0.1 * master)
    return (new_master, new_moment, new_second)


def lane_sum(x):
    parts = [x[:, k * LANES : (k + 1) * LANES] for k in range(x.shape[1] // LANES)]
    while len(parts) > 1:
        parts = [a + b for a, b in zip(parts[::2], parts[1::2])] + ([parts[-1]] if len(parts) % 2 else [])
    return parts[0]


def load_kernel(wanted, t_hbm, cols_hbm, a_hbm, b_hbm, c_hbm, order, t, a, b, c, away, own, cols, sems, small):
    half, width = away.shape
    parts = sems.shape[0]
    copies = []
    for i in range(parts):
        at = pl.ds(i * (width // parts), width // parts)
        copies.append(pltpu.make_async_copy(t_hbm.at[0, :, at], t.at[:, at], sems.at[i]))
    for i, (src, dst) in enumerate(((cols_hbm, cols), (a_hbm, a), (b_hbm, b), (c_hbm, c))):
        copies.append(pltpu.make_async_copy(src, dst, small.at[i]))
    for copy in copies:
        copy.start()
    for copy in copies:
        copy.wait()

    @pl.when(wanted[0] > 0)
    def _():
        slots = b16(jnp.dot(order[...], cols[...], preferred_element_type=jnp.float32))
        for i in range(width // CHUNK):
            at = pl.ds(i * CHUNK, CHUNK)
            term = b16(jnp.dot(slots, t[:, at], preferred_element_type=jnp.float32))
            away[:, at] = term[:half]
            own[:, at] = term[half:]


def stats_kernel(x_hbm, g_hbm, gain, inv_b, k1_b, k0_b, x, g, sems):
    tokens, width = x.shape
    blocks = tokens // ROWBLOCK
    copies = {}
    for b in range(blocks):
        rows = pl.ds(b * ROWBLOCK, ROWBLOCK)
        for k, (src, dst) in enumerate(((x_hbm, x), (g_hbm, g))):
            copies[k, b] = pltpu.make_async_copy(src.at[0, rows], dst.at[rows], sems.at[k, b])
            copies[k, b].start()
    part = 2048
    for b in range(blocks):
        rows = pl.ds(b * ROWBLOCK, ROWBLOCK)
        zero = jnp.zeros((ROWBLOCK, LANES), jnp.float32)
        copies[0, b].wait()

        def first(i, total):
            at = pl.ds(pl.multiple_of(i * part, part), part)
            return total + lane_sum(f32(x[rows, at]))

        mean = jnp.sum(lax.fori_loop(0, width // part, first, zero), axis=1, keepdims=True) / width
        copies[1, b].wait()
        mean_b = jnp.broadcast_to(mean, (ROWBLOCK, LANES))

        def second(i, totals):
            square, scale, cross = totals
            at0 = pl.multiple_of(i * (part // 2), part // 2)
            for k in range(part // 2 // LANES):
                at = pl.ds(at0 + k * LANES, LANES)
                centred = f32(x[rows, at]) - mean_b
                scaled = f32(g[rows, at]) * gain[:, at]
                square = square + centred * centred
                scale = scale + scaled
                cross = cross + scaled * centred
            return square, scale, cross

        square, scale, cross = lax.fori_loop(0, width // (part // 2), second, (zero, zero, zero))
        inv = 1.0 / jnp.sqrt(jnp.sum(square, axis=1, keepdims=True) / width + 1e-05)
        mean_scaled = jnp.sum(scale, axis=1, keepdims=True) / width
        k1 = jnp.sum(cross, axis=1, keepdims=True) / width * inv * inv * inv
        inv_b[rows, :] = jnp.broadcast_to(inv, (ROWBLOCK, LANES))
        k1_b[rows, :] = jnp.broadcast_to(k1, (ROWBLOCK, LANES))
        k0_b[rows, :] = jnp.broadcast_to(mean * k1 - inv * mean_scaled, (ROWBLOCK, LANES))


def norm_term_kernel(gain, inv_b, k1_b, k0_b, x, g, t, order, cols, away, own, passed):
    tokens, width = x.shape
    half = away.shape[0]
    chunks = width // CHUNK

    slots = b16(jnp.dot(order[...], cols[...], preferred_element_type=jnp.float32))

    def fill(i):
        lanes = [pl.ds(i * CHUNK + k * LANES, LANES) for k in range(CHUNK // LANES)]
        gains = [gain[:, at] for at in lanes]
        for r in range(tokens // 16):
            rows = slice(16 * r, 16 * r + 16)
            inv, k1, k0 = inv_b[rows, :], k1_b[rows, :], k0_b[rows, :]
            for k, at in enumerate(lanes):
                inner = f32(g[rows, at]) * gains[k] * inv - f32(x[rows, at]) * k1 + k0
                passed[i % 2, rows, k * LANES : (k + 1) * LANES] = b16(f32(t[rows, at]) + inner)

    def multiply(i):
        at = pl.ds(i * CHUNK, CHUNK)
        term = b16(jnp.dot(slots, passed[i % 2], preferred_element_type=jnp.float32))
        away[:, at] = term[:half]
        own[:, at] = term[half:]

    fill(0)
    for i in range(chunks):
        if i + 1 < chunks:
            fill(i + 1)
        multiply(i)


VMEM = pl.BlockSpec(memory_space=pltpu.VMEM)
HBM = pl.BlockSpec(memory_space=pltpu.HBM)


def loaded_term(wanted, top_grad, cols, state, order):
    _, tokens, width = top_grad.shape
    half = cols.shape[0] // 2
    return pl.pallas_call(
        load_kernel,
        out_shape=[jax.ShapeDtypeStruct((tokens, width), jnp.bfloat16)]
        + [jax.ShapeDtypeStruct(x.shape, x.dtype) for x in state]
        + [jax.ShapeDtypeStruct((half, width), jnp.bfloat16)] * 2,
        in_specs=[pl.BlockSpec(memory_space=pltpu.SMEM), HBM, HBM, HBM, HBM, HBM, VMEM],
        out_specs=[VMEM] * 6,
        scratch_shapes=[
            pltpu.VMEM(cols.shape, cols.dtype), pltpu.SemaphoreType.DMA((4,)), pltpu.SemaphoreType.DMA((4,)),
        ],
        compiler_params=pltpu.CompilerParams(vmem_limit_bytes=56 * 2**20),
        cost_estimate=pl.CostEstimate(flops=128 * tokens * width, bytes_accessed=2 * tokens * width, transcendentals=0),
    )(wanted, top_grad, cols, *state, order)


def norm_stats(ln_input, ln_grad, ln_gain):
    _, tokens, width = ln_input.shape
    return pl.pallas_call(
        stats_kernel,
        out_shape=[jax.ShapeDtypeStruct((tokens, LANES), jnp.float32)] * 3
        + [jax.ShapeDtypeStruct((tokens, width), jnp.bfloat16)] * 2,
        in_specs=[HBM, HBM, VMEM],
        out_specs=[VMEM] * 5,
        scratch_shapes=[pltpu.SemaphoreType.DMA((2, tokens // ROWBLOCK))],
        compiler_params=pltpu.CompilerParams(vmem_limit_bytes=50 * 2**20),
        cost_estimate=pl.CostEstimate(flops=256 * tokens * width, bytes_accessed=4 * tokens * width, transcendentals=0),
    )(ln_input, ln_grad, ln_gain)


def norm_term(ln_gain, stats, order, cols):
    tokens, width = stats[3].shape
    half = cols.shape[0] // 2
    return pl.pallas_call(
        norm_term_kernel,
        out_shape=[jax.ShapeDtypeStruct((half, width), jnp.bfloat16)] * 2,
        in_specs=[VMEM] * 9,
        out_specs=[VMEM, VMEM],
        scratch_shapes=[pltpu.VMEM((2, tokens, CHUNK), jnp.bfloat16)],
        compiler_params=pltpu.CompilerParams(vmem_limit_bytes=20 * 2**20),
        cost_estimate=pl.CostEstimate(flops=128 * tokens * width, bytes_accessed=6 * tokens * width, transcendentals=0),
    )(ln_gain, *stats, order, cols)


def rows_kernel(order, *refs):
    pieces, weights, staged, sems = refs[:-3], refs[-3], refs[-2], refs[-1]
    width = weights.shape[1]
    part = 2048
    copies = []
    for i in range(width // part):
        at = pl.ds(i * part, part)
        slots = jnp.concatenate([piece[:, at] for piece in pieces])
        picked = lax.dot_general(order[...], slots, (((0,), (0,)), ((), ())), preferred_element_type=jnp.float32)
        staged[:, at] = b16(picked)
        copies.append(pltpu.make_async_copy(staged.at[:, at], weights.at[:, at], sems.at[i]))
        copies[-1].start()
    for copy in copies:
        copy.wait()


def rows_in_order(order, pieces):
    rows, width = order.shape[0], pieces[0].shape[1]
    return pl.pallas_call(
        rows_kernel,
        out_shape=jax.ShapeDtypeStruct((rows, width), jnp.bfloat16),
        in_specs=[VMEM] * (1 + len(pieces)),
        out_specs=HBM,
        scratch_shapes=[pltpu.VMEM((rows, width), jnp.bfloat16), pltpu.SemaphoreType.DMA((width // 2048,))],
        compiler_params=pltpu.CompilerParams(vmem_limit_bytes=16 * 2**20),
        cost_estimate=pl.CostEstimate(flops=64 * rows * width, bytes_accessed=4 * rows * width, transcendentals=0),
    )(order, *pieces)


def chip_sum(away, own):
    return f32(own) + f32(permute(away, lambda s, z, y, c: (s, z, y, 1 - c)))


def y_parts(chip):
    chunk = chip.shape[0] // NY
    parts = [chip[:chunk]]
    for j in (2, 1, 3):
        part = b16(chip[j * chunk : (j + 1) * chunk])
        parts.append(permute(part, lambda s, z, y, c, j=j: (s, z, y + j, c)))
    return parts


def summed(parts):
    return f32(parts[0]) + f32(parts[1]) + f32(parts[2]) + f32(parts[3])


def z_sum(line):
    chunk = line.shape[0] // NZ
    total = line[3 * chunk :]
    for k in range(3):
        part = b16(line[k * chunk : (k + 1) * chunk])
        got = permute(part, lambda s, z, y, c, k=k: (s, z ^ FAR[k], y, c))
        total = total + f32(got)
    return total


def update(ln_input, ln_grad, top_grad, ln_gain, hidden, master, moment, second):
    is_last = lax.axis_index("section") == lax.axis_size("section") - 1
    rows, width = hidden.shape[2], master.shape[2]
    own = master.shape[1]
    order = slot_rows(rows)
    own_cols = hidden[0].T
    above = permute(own_cols, lambda s, z, y, c: (s + 1, z, y, c))

    loaded, master, moment, second, away_last, own_last = loaded_term(
        is_last.astype(jnp.int32)[None], top_grad, own_cols, (master, moment, second), order
    )
    other_last = permute(away_last, lambda s, z, y, c: (s, z, y, 1 - c))
    stats = norm_stats(ln_input, ln_grad, ln_gain)

    def main_parts():
        halves = norm_term(ln_gain, (*stats, loaded), order, above)
        return y_parts(chip_sum(*halves))

    def last_section():
        parts_last = y_parts(f32(own_last) + f32(other_last))
        mine, *others = main_parts()
        mine, *parts_last = lax.optimization_barrier((mine, *parts_last))
        grad = z_sum(summed(parts_last))
        return b16(summed([mine, *others])), grad

    def other_section():
        return b16(summed(main_parts())), jnp.zeros((own, width), jnp.float32)

    line, grad_last = lax.cond(is_last, last_section, other_section)
    grad = jnp.zeros((own, width), jnp.float32)
    for k in range(NZ):
        grad = grad + f32(
            permute(line[k * own : (k + 1) * own], lambda s, z, y, c, k=k: (s - 1, z ^ FAR[k], y, c))
        )
    grad = jnp.where(is_last, grad_last, grad)
    new_master, new_moment, new_second = adam_update(grad, master[0], moment[0], second[0])
    piece = b16(new_master)
    piece = jnp.concatenate([permute(piece, lambda s, z, y, c: (s, z ^ 3, y, c)), piece])
    piece = jnp.concatenate([permute(piece, lambda s, z, y, c: (s, z ^ 1, y, c)), piece])

    def swap(x):
        return permute(x, lambda s, z, y, c: (s, z, y, 1 - c))

    half = {0: piece}
    for j in (2, 1, 3):
        half[j] = permute(piece, lambda s, z, y, c, j=j: (s, z, y - j, c))
    other = {j: swap(half[j]) for j in (0, 2, 1, 3)}
    weights = rows_in_order(order, [other[j] for j in range(NY)] + [half[j] for j in range(NY)])
    return (new_master[None], new_moment[None], new_second[None], weights[None])


def solution(mesh):
    finer = Mesh(mesh.devices.reshape(mesh.shape["section"], NZ, NY, NC), AXES)
    tokens = P("section", DP, None)
    return jax.shard_map(
        update,
        mesh=finer,
        in_specs=(tokens, tokens, tokens, P("section", None), tokens, tokens, tokens, tokens),
        out_specs=(tokens, tokens, tokens, P("section", None, None)),
        check_vma=False,
    )
```

time: 100 us -> 95.4 us (0.954)
  the two profiles are of different devices: /device:TPU:37 before, /device:TPU:5 now
where the time goes in v2:
time: 95.4 us; the launch traced here: 95.3 us
  starting transfers between devices  51.9 us (54%)
  waiting for transfers between devices  26.3 us (28%)
  Pallas kernels  11.9 us (12%)
  other arithmetic  3.66 us (4%)
  between operations  0.99 us (1%)
    ppermute x19, starting transfers between devices, permute(): return lax.ppermute(value, AXES, pairs)  51.9 us
    ppermute x19, waiting for transfers between devices, permute(): return lax.ppermute(value, AXES, pairs)  26.3 us
    pallas_call x1, Pallas kernels, norm_stats(): pl.pallas_call(stats_kernel, out_shape=[jax.ShapeDtypeStruct((tokens, LAN...  4.41 us
    pallas_call x1, Pallas kernels, loaded_term(): pl.pallas_call(load_kernel, out_shape=[jax.ShapeDtypeStruct((tokens, widt...  3.13 us
    pallas_call x1, Pallas kernels, norm_term(): pl.pallas_call(norm_term_kernel, out_shape=[jax.ShapeDtypeStruct((half, w...  2.97 us
    convert_element_type x1, other arithmetic, b16(): return x.astype(jnp.bfloat16)  2.05 us
  transfers between devices with their start and end apart: 19, of which 8 were waited for; matrix products, arithmetic and copies ran while one was open for 1% of the time, Pallas kernels for 5%

profile of v2, /device:TPU:5, one launch (start us, length us, event | category | flops | bytes accessed | tf_op | source)
XLA Modules:
  0.0 95.3 jit_solution(8576859730649810971)
XLA Ops:
  0.7 0.2 fusion.20.order
  0.9 0.0 copy-start.4
  0.9 0.0 copy-start
  0.9 0.0 copy-start.1
  0.9 3.1 %shard_map.111 = (bf16[128,12288]{1,0:T(8,128)(2,1)S(1)}, f32[1,2,12288]{2,1,0:T(2,128)}, f32[1,2,12288]{2,1,0:T(2,128)}, f32[1,2,12288]{2,1,0:T(2,128)}, bf16[3...) custom-call(s32[1]{0:T(128)} %bitcast.wanted, bf16[1,128,12288]{2,1,0:T(8,128)(2,1)} %t_hbm.1, ...), custom_call_target="tpu_custom_call" | custom-call | flops 201326592 | bytes 3145728 | tf_op jit(solution)/shard_map/pallas_call | solution.py:177
  4.1 0.8 collective-permute-start.15
  4.8 0.0 copy-done.4
  4.8 0.9 collective-permute-start.14
  5.7 0.0 copy-done
  5.8 0.0 copy-done.1
  5.8 4.4 %shard_map.112 = (f32[128,128]{1,0:T(8,128)S(1)}, f32[128,128]{1,0:T(8,128)S(1)}, f32[128,128]{1,0:T(8,128)S(1)}, bf16[128,12288]{1,0:T(8,128)(2,1)S(1)}, bf16[128,12288]{1,0:T(8,128)(2,1)S(1)}) custom-call(bf16[1,128,12288]{2,1,0:T(8,128)(2,1)S(1)} %copy-done, bf16[1,128,12288]{2,1,0:T(8,128)(2,1)} %g_hbm.1, f32[1,12288]{1,0:T(1,128)S(1)} %copy-done.1), custom_call_target="tpu_custom_call" | custom-call | flops 402653184 | bytes 6291456 | tf_op jit(solution)/shard_map/pallas_call | solution.py:194
  10.2 0.0 collective-permute-done.14
  10.2 0.0 collective-permute-done.15
  10.2 19.0 %conditional.2 = (bf16[8,12288]{1,0:T(8,128)(2,1)S(1)}, f32[2,12288]{1,0:T(2,128)S(1)}) conditional(s32[]{:T(128)} %convert_element_type.93, (f32[1,12288]{1,0:T(1,128)S(1)}, f32[128,128]{1,0:T(8,128)S(1)}, f32[128,128]{1,0:T(8,128)S(1)}, f32[128,128]{1,0:T(8,128)S(1)}, bf16[128,12288]{1,0:T(8,128)(2,1)S(1)}, ...), branch_computations={%region_0.1_spmd, %region_1.2_spmd} | conditional | flops 205996032 | bytes 33079712
  10.2 3.0 %branch_0_fun.1 = (bf16[32,12288]{1,0:T(8,128)(2,1)S(1)}, bf16[32,12288]{1,0:T(8,128)(2,1)S(1)}) custom-call(f32[1,12288]{1,0:T(1,128)S(1)} %get-tuple-element.43.gain, f32[128,128]{1,0:T(8,128)S(1)} %get-tuple-element.44.inv_b, f32[128,128]{1,0:T(8,128)S(1)} %get-tuple-element.45.k1_b, f32[128,128]{1,0:T(8,128)S(1)} %get-tuple-element.46.k0_b, ...), custom_call_target="tpu_custom_call" | custom-call | flops 201326592 | bytes 9437184 | tf_op jit(solution)/shard_map/cond/branch_0_fun/pallas_call | solution.py:209
  13.2 0.5 collective-permute-start
  13.6 1.9 %collective-permute-done = bf16[32,12288]{1,0:T(8,128)(2,1)S(1)} collective-permute-done((bf16[32,12288]{1,0:T(8,128)(2,1)S(1)}, bf16[32,12288]{1,0:T(8,128)(2,1)S(1)}, u32[]{:S(2)}, u32[]{:S(2)}) %collective-permute-start) | collective-permute-done | bytes 786464 | tf_op jit(solution)/shard_map/cond/branch_0_fun/ppermute | solution.py:29
  15.6 0.2 fusion.2
  15.8 2.8 %collective-permute-start.3 = (bf16[8,12288]{1,0:T(8,128)(2,1)S(1)}, bf16[8,12288]{1,0:T(8,128)(2,1)S(1)}, u32[]{:S(2)}, u32[]{:S(2)}) collective-permute-start(bf16[8,12288]{1,0:T(8,128)(2,1)S(1)} %get-tuple-element.110), channel_id=1, source_target_pairs={{0,6},{1,7},{2,0},{3,1},{4,2},{5,3},{6,4},{7,5},{8,14},{9,15},{10,... | collective-permute-start | bytes 589832 | tf_op jit(solution)/shard_map/cond/branch_0_fun/ppermute | solution.py:29
  18.6 0.0 collective-permute-start.2
  18.6 1.6 %collective-permute-start.1 = (bf16[8,12288]{1,0:T(8,128)(2,1)S(1)}, bf16[8,12288]{1,0:T(8,128)(2,1)S(1)}, u32[]{:S(2)}, u32[]{:S(2)}) collective-permute-start(bf16[8,12288]{1,0:T(8,128)(2,1)S(1)} %get-tuple-element.109), channel_id=1, source_target_pairs={{0,4},{1,5},{2,6},{3,7},{4,0},{5,1},{6,2},{7,3},{8,12},{9,13},{10,... | collective-permute-start | bytes 589832 | tf_op jit(solution)/shard_map/cond/branch_0_fun/ppermute | solution.py:29
  20.3 2.1 %collective-permute-done.3 = bf16[8,12288]{1,0:T(8,128)(2,1)S(1)} collective-permute-done((bf16[8,12288]{1,0:T(8,128)(2,1)S(1)}, bf16[8,12288]{1,0:T(8,128)(2,1)S(1)}, u32[]{:S(2)}, u32[]{:S(2)}) %collective-permute-start.3) | collective-permute-done | bytes 196640 | tf_op jit(solution)/shard_map/cond/branch_0_fun/ppermute | solution.py:29
  22.4 4.3 %collective-permute-done.2 = bf16[8,12288]{1,0:T(8,128)(2,1)S(1)} collective-permute-done((bf16[8,12288]{1,0:T(8,128)(2,1)S(1)}, bf16[8,12288]{1,0:T(8,128)(2,1)S(1)}, u32[]{:S(2)}, u32[]{:S(2)}) %collective-permute-start.2) | collective-permute-done | bytes 196640 | tf_op jit(solution)/shard_map/cond/branch_0_fun/ppermute | solution.py:29
  26.7 2.2 %collective-permute-done.1 = bf16[8,12288]{1,0:T(8,128)(2,1)S(1)} collective-permute-done((bf16[8,12288]{1,0:T(8,128)(2,1)S(1)}, bf16[8,12288]{1,0:T(8,128)(2,1)S(1)}, u32[]{:S(2)}, u32[]{:S(2)}) %collective-permute-start.1) | collective-permute-done | bytes 196640 | tf_op jit(solution)/shard_map/cond/branch_0_fun/ppermute | solution.py:29
  28.9 0.1 fusion.1
  29.2 0.0 copy-start.2
  29.2 0.0 copy-start.3
  29.3 0.1 fusion.30
  29.4 0.6 collective-permute-start.19
  30.0 6.0 %collective-permute-start.18 = (bf16[2,12288]{1,0:T(2,128)(2,1)S(1)}, bf16[2,12288]{1,0:T(2,128)(2,1)S(1)}, u32[]{:S(2)}, u32[]{:S(2)}) collective-permute-start(bf16[2,12288]{1,0:T(2,128)(2,1)S(1)} %get-tuple-element.126), channel_id=1, source_target_pairs={{0,248},{1,249},{2,250},{3,251},{4,252},{5,253},{6,254},{7,255},{8... | collective-permute-start | bytes 147464 | tf_op jit(solution)/shard_map/ppermute | solution.py:29
  36.0 18.8 %collective-permute-start.17 = (bf16[2,12288]{1,0:T(2,128)(2,1)S(1)}, bf16[2,12288]{1,0:T(2,128)(2,1)S(1)}, u32[]{:S(2)}, u32[]{:S(2)}) collective-permute-start(bf16[2,12288]{1,0:T(2,128)(2,1)S(1)} %get-tuple-element.127), channel_id=1, source_target_pairs={{0,232},{1,233},{2,234},{3,235},{4,236},{5,237},{6,238},{7,239},{8... | collective-permute-start | bytes 147464 | tf_op jit(solution)/shard_map/ppermute | solution.py:29
  54.8 1.1 %collective-permute-start.16 = (bf16[2,12288]{1,0:T(2,128)(2,1)S(1)}, bf16[2,12288]{1,0:T(2,128)(2,1)S(1)}, u32[]{:S(2)}, u32[]{:S(2)}) collective-permute-start(bf16[2,12288]{1,0:T(2,128)(2,1)S(1)} %get-tuple-element.125), channel_id=1, source_target_pairs={{0,240},{1,241},{2,242},{3,243},{4,244},{5,245},{6,246},{7,247},{8... | collective-permute-start | bytes 147464 | tf_op jit(solution)/shard_map/ppermute | solution.py:29
  56.0 0.0 collective-permute-done.19
  56.0 0.0 collective-permute-done.18
  56.0 0.0 collective-permute-done.17
  56.0 6.9 %collective-permute-done.16 = bf16[2,12288]{1,0:T(2,128)(2,1)S(1)} collective-permute-done((bf16[2,12288]{1,0:T(2,128)(2,1)S(1)}, bf16[2,12288]{1,0:T(2,128)(2,1)S(1)}, u32[]{:S(2)}, u32[]{:S(2)}) %collective-permute-start.16) | collective-permute-done | bytes 49184 | tf_op jit(solution)/shard_map/ppermute | solution.py:29
  62.9 2.1 %fusion.25 = (bf16[2,12288]{1,0:T(2,128)(2,1)S(1)}, f32[2,12288]{1,0:T(2,128)}, f32[2,12288]{1,0:T(2,128)S(1)}) fusion(f32[1,2,12288]{2,1,0:T(2,128)} %get-tuple-element.101, f32[1,2,12288]{2,1,0:T(2,128)} %get-tuple-element.90, f32[1,2,12288]{2,1,0:T(2,128)} %get-tuple-element.89, f32[2,12288]{1,0:T(2,128)S(1)} %get-tuple-element.99, ...), kind=kLoop, calls=%fused_computation.67 | loop fusion | flops 589824 | bytes 835585 | tf_op jit(solution)/shard_map/convert_element_type | solution.py:52
  65.0 0.0 collective-permute-start.20
  65.0 5.0 %collective-permute-done.20 = bf16[2,12288]{1,0:T(2,128)(2,1)S(1)} collective-permute-done((bf16[2,12288]{1,0:T(2,128)(2,1)S(1)}, bf16[2,12288]{1,0:T(2,128)(2,1)S(1)}, u32[]{:S(2)}, u32[]{:S(2)}) %collective-permute-start.20) | collective-permute-done | bytes 49184 | tf_op jit(solution)/shard_map/ppermute | solution.py:29
  70.0 0.1 pad_maximum_fusion.1
  70.2 0.9 collective-permute-start.21
  71.1 3.6 %collective-permute-done.21 = bf16[4,12288]{1,0:T(4,128)(2,1)S(1)} collective-permute-done((bf16[4,12288]{1,0:T(4,128)(2,1)S(1)}, bf16[4,12288]{1,0:T(4,128)(2,1)S(1)}, u32[]{:S(2)}, u32[]{:S(2)}) %collective-permute-start.21) | collective-permute-done | bytes 98336 | tf_op jit(solution)/shard_map/ppermute | solution.py:29
  74.6 0.2 pad_maximum_fusion.refs_4_
  74.8 0.1 collective-permute-start.23
  74.9 2.6 %collective-permute-start.25 = (bf16[8,12288]{1,0:T(8,128)(2,1)S(1)}, bf16[8,12288]{1,0:T(8,128)(2,1)S(1)}, u32[]{:S(2)}, u32[]{:S(2)}) collective-permute-start(bf16[8,12288]{1,0:T(8,128)(2,1)S(1)} %pad_maximum_fusion.refs_4_), channel_id=1, source_target_pairs={{0,4},{1,5},{2,6},{3,7},{4,0},{5,1},{6,2},{7,3},{8,12},{9,13},{10,... | collective-permute-start | bytes 589832 | tf_op jit(solution)/shard_map/ppermute | solution.py:29
  77.5 0.8 collective-permute-start.27
  78.3 6.9 %collective-permute-start.22 = (bf16[8,12288]{1,0:T(8,128)(2,1)S(1)}, bf16[8,12288]{1,0:T(8,128)(2,1)S(1)}, u32[]{:S(2)}, u32[]{:S(2)}) collective-permute-start(bf16[8,12288]{1,0:T(8,128)(2,1)S(1)} %pad_maximum_fusion.refs_4_), channel_id=1, source_target_pairs={{0,1},{1,0},{2,3},{3,2},{4,5},{5,4},{6,7},{7,6},{8,9},{9,8},{10,11... | collective-permute-start | bytes 589832 | tf_op jit(solution)/shard_map/ppermute | solution.py:29
  85.1 0.0 collective-permute-done.23.refs_5_
  85.1 3.6 %collective-permute-start.24 = (bf16[8,12288]{1,0:T(8,128)(2,1)S(1)}, bf16[8,12288]{1,0:T(8,128)(2,1)S(1)}, u32[]{:S(2)}, u32[]{:S(2)}) collective-permute-start(bf16[8,12288]{1,0:T(8,128)(2,1)S(1)} %collective-permute-done.23.refs_5_), channel_id=1, source_target_pairs={{0,1},{1,0},{2,3},{3,2},{4,5},{5,4},{6,7},{7,6},{8,9},{9,8},{10,11... | collective-permute-start | bytes 589832 | tf_op jit(solution)/shard_map/ppermute | solution.py:29
  88.8 0.0 collective-permute-done.25.refs_6_
  88.8 1.8 %collective-permute-start.26 = (bf16[8,12288]{1,0:T(8,128)(2,1)S(1)}, bf16[8,12288]{1,0:T(8,128)(2,1)S(1)}, u32[]{:S(2)}, u32[]{:S(2)}) collective-permute-start(bf16[8,12288]{1,0:T(8,128)(2,1)S(1)} %collective-permute-done.25.refs_6_), channel_id=1, source_target_pairs={{0,1},{1,0},{2,3},{3,2},{4,5},{5,4},{6,7},{7,6},{8,9},{9,8},{10,11... | collective-permute-start | bytes 589832 | tf_op jit(solution)/shard_map/ppermute | solution.py:29
  90.6 0.0 collective-permute-done.27.refs_7_
  90.6 2.0 %collective-permute-start.28 = (bf16[8,12288]{1,0:T(8,128)(2,1)S(1)}, bf16[8,12288]{1,0:T(8,128)(2,1)S(1)}, u32[]{:S(2)}, u32[]{:S(2)}) collective-permute-start(bf16[8,12288]{1,0:T(8,128)(2,1)S(1)} %collective-permute-done.27.refs_7_), channel_id=1, source_target_pairs={{0,1},{1,0},{2,3},{3,2},{4,5},{5,4},{6,7},{7,6},{8,9},{9,8},{10,11... | collective-permute-start | bytes 589832 | tf_op jit(solution)/shard_map/ppermute | solution.py:29
  92.6 0.0 copy-done.2
  92.6 0.0 copy-done.3
  92.6 0.8 fusion.23
  93.4 0.0 collective-permute-done.22.refs_0_
  93.4 0.0 collective-permute-done.24.refs_1_
  93.4 0.0 collective-permute-done.26.refs_2_
  93.4 0.2 collective-permute-done.28.refs_3_
  93.7 1.4 %shard_map.113 = bf16[64,12288]{1,0:T(8,128)(2,1)} custom-call(bf16[64,64]{1,0:T(8,128)(2,1)S(1)} %fusion.20.order, bf16[8,12288]{1,0:T(8,128)(2,1)S(1)} %collective-permute-done.22.refs_0_, bf16[8,12288]{1,0:T(8,128)(2,1)S(1)} %collective-permute-done.24.refs_1_, bf16[8,12288]{1,0:T(8,128)(2,1)S(1)} %collective-permute-done.26.refs_2_, ...), custom_call_target="tpu_custom_call" | custom-call | flops 50331648 | bytes 3145728 | tf_op jit(solution)/shard_map/pallas_call | solution.py:238
  (8 shorter events, 0.1 us)
Async XLA Ops:
  0.9 3.9 %copy-start.4 = (bf16[1,128,64]{1,2,0:T(8,128)(2,1)S(1)}, bf16[1,128,64]{1,2,0:T(8,128)(2,1)}, u32[]{:S(2)}) copy-start(bf16[1,128,64]{1,2,0:T(8,128)(2,1)} %param.14) | copy-start | bytes 49156
  0.9 4.8 %copy-start = (bf16[1,128,12288]{2,1,0:T(8,128)(2,1)S(1)}, bf16[1,128,12288]{2,1,0:T(8,128)(2,1)}, u32[]{:S(2)}) copy-start(bf16[1,128,12288]{2,1,0:T(8,128)(2,1)} %x_hbm.1) | copy-start | bytes 9437188
  0.9 4.8 %copy-start.1 = (f32[1,12288]{1,0:T(1,128)S(1)}, f32[1,12288]{1,0:T(1,128)}, u32[]{:S(2)}) copy-start(f32[1,12288]{1,0:T(1,128)} %gain.1) | copy-start | bytes 147460
  4.1 6.1 %collective-permute-start.15 = (bf16[32,12288]{1,0:T(8,128)(2,1)}, bf16[32,12288]{1,0:T(8,128)(2,1)S(1)}, u32[]{:S(2)}, u32[]{:S(2)}) collective-permute-start(bf16[32,12288]{1,0:T(8,128)(2,1)} %get-tuple-element.98), channel_id=1, source_target_pairs={{0,1},{1,0},{2,3},{3,2},{4,5},{5,4},{6,7},{7,6},{8,9},{9,8},{10,11... | collective-permute-start | bytes 2359304 | tf_op jit(solution)/shard_map/ppermute | solution.py:29
  4.8 5.3 %collective-permute-start.14 = (bf16[64,128]{1,0:T(8,128)(2,1)S(1)}, bf16[64,128]{1,0:T(8,128)(2,1)S(1)}, u32[]{:S(2)}, u32[]{:S(2)}) collective-permute-start(bf16[64,128]{1,0:T(8,128)(2,1)S(1)} %bitcast.37), channel_id=1, source_target_pairs={{0,32},{1,33},{2,34},{3,35},{4,36},{5,37},{6,38},{7,39},{8,40},{9,... | collective-permute-start | bytes 49160 | tf_op jit(solution)/shard_map/ppermute | solution.py:29
  13.2 2.4 %collective-permute-start = (bf16[32,12288]{1,0:T(8,128)(2,1)S(1)}, bf16[32,12288]{1,0:T(8,128)(2,1)S(1)}, u32[]{:S(2)}, u32[]{:S(2)}) collective-permute-start(bf16[32,12288]{1,0:T(8,128)(2,1)S(1)} %get-tuple-element.53), channel_id=1, source_target_pairs={{0,1},{1,0},{2,3},{3,2},{4,5},{5,4},{6,7},{7,6},{8,9},{9,8},{10,11... | collective-permute-start | bytes 2359304 | tf_op jit(solution)/shard_map/cond/branch_0_fun/ppermute | solution.py:29
  15.8 6.6 %collective-permute-start.3 = (bf16[8,12288]{1,0:T(8,128)(2,1)S(1)}, bf16[8,12288]{1,0:T(8,128)(2,1)S(1)}, u32[]{:S(2)}, u32[]{:S(2)}) collective-permute-start(bf16[8,12288]{1,0:T(8,128)(2,1)S(1)} %get-tuple-element.110), channel_id=1, source_target_pairs={{0,6},{1,7},{2,0},{3,1},{4,2},{5,3},{6,4},{7,5},{8,14},{9,15},{10,... | collective-permute-start | bytes 589832 | tf_op jit(solution)/shard_map/cond/branch_0_fun/ppermute | solution.py:29
  18.6 8.0 %collective-permute-start.2 = (bf16[8,12288]{1,0:T(8,128)(2,1)S(1)}, bf16[8,12288]{1,0:T(8,128)(2,1)S(1)}, u32[]{:S(2)}, u32[]{:S(2)}) collective-permute-start(bf16[8,12288]{1,0:T(8,128)(2,1)S(1)} %get-tuple-element.111), channel_id=1, source_target_pairs={{0,2},{1,3},{2,4},{3,5},{4,6},{5,7},{6,0},{7,1},{8,10},{9,11},{10,... | collective-permute-start | bytes 589832 | tf_op jit(solution)/shard_map/cond/branch_0_fun/ppermute | solution.py:29
  18.6 10.2 %collective-permute-start.1 = (bf16[8,12288]{1,0:T(8,128)(2,1)S(1)}, bf16[8,12288]{1,0:T(8,128)(2,1)S(1)}, u32[]{:S(2)}, u32[]{:S(2)}) collective-permute-start(bf16[8,12288]{1,0:T(8,128)(2,1)S(1)} %get-tuple-element.109), channel_id=1, source_target_pairs={{0,4},{1,5},{2,6},{3,7},{4,0},{5,1},{6,2},{7,3},{8,12},{9,13},{10,... | collective-permute-start | bytes 589832 | tf_op jit(solution)/shard_map/cond/branch_0_fun/ppermute | solution.py:29
  29.2 63.4 %copy-start.2 = (f32[1,2,12288]{2,1,0:T(2,128)S(1)}, f32[1,2,12288]{2,1,0:T(2,128)}, u32[]{:S(2)}) copy-start(f32[1,2,12288]{2,1,0:T(2,128)} %get-tuple-element.90) | copy-start | bytes 294916
  29.2 63.4 %copy-start.3 = (f32[1,2,12288]{2,1,0:T(2,128)S(1)}, f32[1,2,12288]{2,1,0:T(2,128)}, u32[]{:S(2)}) copy-start(f32[1,2,12288]{2,1,0:T(2,128)} %get-tuple-element.101) | copy-start | bytes 294916
  29.4 26.6 %collective-permute-start.19 = (bf16[2,12288]{1,0:T(2,128)(2,1)S(1)}, bf16[2,12288]{1,0:T(2,128)(2,1)S(1)}, u32[]{:S(2)}, u32[]{:S(2)}) collective-permute-start(bf16[2,12288]{1,0:T(2,128)(2,1)S(1)} %get-tuple-element.128), channel_id=1, source_target_pairs={{0,224},{1,225},{2,226},{3,227},{4,228},{5,229},{6,230},{7,231},{8... | collective-permute-start | bytes 147464 | tf_op jit(solution)/shard_map/ppermute | solution.py:29
  30.0 25.9 %collective-permute-start.18 = (bf16[2,12288]{1,0:T(2,128)(2,1)S(1)}, bf16[2,12288]{1,0:T(2,128)(2,1)S(1)}, u32[]{:S(2)}, u32[]{:S(2)}) collective-permute-start(bf16[2,12288]{1,0:T(2,128)(2,1)S(1)} %get-tuple-element.126), channel_id=1, source_target_pairs={{0,248},{1,249},{2,250},{3,251},{4,252},{5,253},{6,254},{7,255},{8... | collective-permute-start | bytes 147464 | tf_op jit(solution)/shard_map/ppermute | solution.py:29
  36.0 20.0 %collective-permute-start.17 = (bf16[2,12288]{1,0:T(2,128)(2,1)S(1)}, bf16[2,12288]{1,0:T(2,128)(2,1)S(1)}, u32[]{:S(2)}, u32[]{:S(2)}) collective-permute-start(bf16[2,12288]{1,0:T(2,128)(2,1)S(1)} %get-tuple-element.127), channel_id=1, source_target_pairs={{0,232},{1,233},{2,234},{3,235},{4,236},{5,237},{6,238},{7,239},{8... | collective-permute-start | bytes 147464 | tf_op jit(solution)/shard_map/ppermute | solution.py:29
  54.8 8.1 %collective-permute-start.16 = (bf16[2,12288]{1,0:T(2,128)(2,1)S(1)}, bf16[2,12288]{1,0:T(2,128)(2,1)S(1)}, u32[]{:S(2)}, u32[]{:S(2)}) collective-permute-start(bf16[2,12288]{1,0:T(2,128)(2,1)S(1)} %get-tuple-element.125), channel_id=1, source_target_pairs={{0,240},{1,241},{2,242},{3,243},{4,244},{5,245},{6,246},{7,247},{8... | collective-permute-start | bytes 147464 | tf_op jit(solution)/shard_map/ppermute | solution.py:29
  65.0 5.0 %collective-permute-start.20 = (bf16[2,12288]{1,0:T(2,128)(2,1)S(1)}, bf16[2,12288]{1,0:T(2,128)(2,1)S(1)}, u32[]{:S(2)}, u32[]{:S(2)}) collective-permute-start(bf16[2,12288]{1,0:T(2,128)(2,1)S(1)} %get-tuple-element.104), channel_id=1, source_target_pairs={{0,24},{1,25},{2,26},{3,27},{4,28},{5,29},{6,30},{7,31},{8,16},{9,... | collective-permute-start | bytes 147464 | tf_op jit(solution)/shard_map/ppermute | solution.py:29
  70.2 4.5 %collective-permute-start.21 = (bf16[4,12288]{1,0:T(4,128)(2,1)S(1)}, bf16[4,12288]{1,0:T(4,128)(2,1)S(1)}, u32[]{:S(2)}, u32[]{:S(2)}) collective-permute-start(bf16[4,12288]{1,0:T(4,128)(2,1)S(1)} %pad_maximum_fusion.1), channel_id=1, source_target_pairs={{0,8},{1,9},{2,10},{3,11},{4,12},{5,13},{6,14},{7,15},{8,0},{9,1},... | collective-permute-start | bytes 294920 | tf_op jit(solution)/shard_map/ppermute | solution.py:29
  74.8 10.4 %collective-permute-start.23 = (bf16[8,12288]{1,0:T(8,128)(2,1)S(1)}, bf16[8,12288]{1,0:T(8,128)(2,1)S(1)}, u32[]{:S(2)}, u32[]{:S(2)}) collective-permute-start(bf16[8,12288]{1,0:T(8,128)(2,1)S(1)} %pad_maximum_fusion.refs_4_), channel_id=1, source_target_pairs={{0,6},{1,7},{2,0},{3,1},{4,2},{5,3},{6,4},{7,5},{8,14},{9,15},{10,... | collective-permute-start | bytes 589832 | tf_op jit(solution)/shard_map/ppermute | solution.py:29
  74.9 13.9 %collective-permute-start.25 = (bf16[8,12288]{1,0:T(8,128)(2,1)S(1)}, bf16[8,12288]{1,0:T(8,128)(2,1)S(1)}, u32[]{:S(2)}, u32[]{:S(2)}) collective-permute-start(bf16[8,12288]{1,0:T(8,128)(2,1)S(1)} %pad_maximum_fusion.refs_4_), channel_id=1, source_target_pairs={{0,4},{1,5},{2,6},{3,7},{4,0},{5,1},{6,2},{7,3},{8,12},{9,13},{10,... | collective-permute-start | bytes 589832 | tf_op jit(solution)/shard_map/ppermute | solution.py:29
  77.5 13.1 %collective-permute-start.27 = (bf16[8,12288]{1,0:T(8,128)(2,1)S(1)}, bf16[8,12288]{1,0:T(8,128)(2,1)S(1)}, u32[]{:S(2)}, u32[]{:S(2)}) collective-permute-start(bf16[8,12288]{1,0:T(8,128)(2,1)S(1)} %pad_maximum_fusion.refs_4_), channel_id=1, source_target_pairs={{0,2},{1,3},{2,4},{3,5},{4,6},{5,7},{6,0},{7,1},{8,10},{9,11},{10,... | collective-permute-start | bytes 589832 | tf_op jit(solution)/shard_map/ppermute | solution.py:29
  78.3 15.2 %collective-permute-start.22 = (bf16[8,12288]{1,0:T(8,128)(2,1)S(1)}, bf16[8,12288]{1,0:T(8,128)(2,1)S(1)}, u32[]{:S(2)}, u32[]{:S(2)}) collective-permute-start(bf16[8,12288]{1,0:T(8,128)(2,1)S(1)} %pad_maximum_fusion.refs_4_), channel_id=1, source_target_pairs={{0,1},{1,0},{2,3},{3,2},{4,5},{5,4},{6,7},{7,6},{8,9},{9,8},{10,11... | collective-permute-start | bytes 589832 | tf_op jit(solution)/shard_map/ppermute | solution.py:29
  85.1 8.3 %collective-permute-start.24 = (bf16[8,12288]{1,0:T(8,128)(2,1)S(1)}, bf16[8,12288]{1,0:T(8,128)(2,1)S(1)}, u32[]{:S(2)}, u32[]{:S(2)}) collective-permute-start(bf16[8,12288]{1,0:T(8,128)(2,1)S(1)} %collective-permute-done.23.refs_5_), channel_id=1, source_target_pairs={{0,1},{1,0},{2,3},{3,2},{4,5},{5,4},{6,7},{7,6},{8,9},{9,8},{10,11... | collective-permute-start | bytes 589832 | tf_op jit(solution)/shard_map/ppermute | solution.py:29
  88.8 4.7 %collective-permute-start.26 = (bf16[8,12288]{1,0:T(8,128)(2,1)S(1)}, bf16[8,12288]{1,0:T(8,128)(2,1)S(1)}, u32[]{:S(2)}, u32[]{:S(2)}) collective-permute-start(bf16[8,12288]{1,0:T(8,128)(2,1)S(1)} %collective-permute-done.25.refs_6_), channel_id=1, source_target_pairs={{0,1},{1,0},{2,3},{3,2},{4,5},{5,4},{6,7},{7,6},{8,9},{9,8},{10,11... | collective-permute-start | bytes 589832 | tf_op jit(solution)/shard_map/ppermute | solution.py:29
  90.6 3.1 %collective-permute-start.28 = (bf16[8,12288]{1,0:T(8,128)(2,1)S(1)}, bf16[8,12288]{1,0:T(8,128)(2,1)S(1)}, u32[]{:S(2)}, u32[]{:S(2)}) collective-permute-start(bf16[8,12288]{1,0:T(8,128)(2,1)S(1)} %collective-permute-done.27.refs_7_), channel_id=1, source_target_pairs={{0,1},{1,0},{2,3},{3,2},{4,5},{5,4},{6,7},{7,6},{8,9},{9,8},{10,11... | collective-permute-start | bytes 589832 | tf_op jit(solution)/shard_map/ppermute | solution.py:29
